TPU v7x, 512 devices: a 4x2x32 block of a 4x8x32 slice. The times are simulated.
512 devices in a mesh: groups: 2 (over y), blk: 32 (over z), head: 4 (over x), pair: 2 (over core).
Axes of the slice: x: 4, y: 2, z: 32, core: 2. Of those that a mesh axis runs over, the one named last changes fastest.
The devices are a block of a 4x8x32 slice.
Arguments:
- single: bfloat16 [2048, 384], P(('groups', 'blk')), parts along dimension 0, may hold values from -6 to 6
- pair: bfloat16 [2048, 32, 32, 128], P(('groups', 'blk'), None, 'pair'), parts along dimension 0, may hold values from -6 to 6
- frames: float32 [12, 2048], P(None, ('groups', 'blk')), parts along dimension 1, as said below
- chain: int32 [2048], P(('groups', 'blk')), parts along dimension 0, may hold values from 0 to 5, never falling along the last dimension, each value on 1 to 341 neighbouring positions
- mask: int32 [2048], P(('groups', 'blk')), parts along dimension 0, may hold values 0 or 1
- w_query: bfloat16 [384, 192], P(None, 'head'), may hold values from -0.3125 to 0.3125
- w_key_value: bfloat16 [384, 384], P(None, 'head'), may hold values from -0.3125 to 0.3125
- w_query_points: bfloat16 [384, 144], P(None, 'head'), may hold values from -0.3125 to 0.3125
- w_kv_points: bfloat16 [384, 432], P(None, 'head'), may hold values from -0.3125 to 0.3125
- w_pair_bias: bfloat16 [128, 12], P(None, 'head'), may hold values from -0.5 to 0.5
- head_weights: float32 [12], P('head'), may hold values from -9 to 1
- chain_bias: float32 [12], P('head'), may hold values from -3 to 3
- w_out: bfloat16 [12, 176, 384], P('head'), may hold values from -0.125 to 0.125
- out_gain: float32 [384], replicated, may hold values from 0.5 to 1.5
- w_backbone: bfloat16 [384, 6], replicated, may hold values from -0.3125 to 0.3125
Outputs:
- single_out: bfloat16 [2048, 384], P(('groups', 'blk')), parts along dimension 0
- frames_out: float32 [12, 2048], P(None, 'groups'), parts along dimension 1
There are 2 independent parts, one for each index of `groups`. A program takes and returns all parts, laid end to end along the dimension named above; an argument that names none is the same for every part. Nothing has to cross between parts.
Inputs may be any that keep to these rules, and one draw needn't show every extreme that they name: `frames`: rows 0 to 8 of every column hold an orthonormal rotation matrix row by row; rows 9 to 11 the translation.
All inputs are finite; a program needn't handle non-finite values. No bound on the sum of `mask` on one device may be relied on, other than what follows from the above.
Results may differ from a plain program's by a relative error of at most 0.0048.
Values sent between devices are 32-bit elements; how exact they have to be, the bound alone decides.
A program may use at most 64 MiB of HBM per device.

v0:
```python
import math

import jax
import jax.numpy as jnp
from jax import lax
from jax.sharding import PartitionSpec as P

HIGH = lax.Precision.HIGHEST
LOGIT_WEIGHT = math.sqrt(1.0 / 3.0)
MASK_PENALTY = 100000.0


def side_by_side(arrays, axis, dim, along):
    widths = [a.shape[along] for a in arrays]
    both = jnp.concatenate(arrays, axis=along)
    out = lax.all_gather(both, axis, axis=dim, tiled=True)
    return tuple(jnp.split(out, [sum(widths[:k]) for k in range(1, len(widths))], axis=along))


def copy_for_each(array, axis):
    copies = jnp.broadcast_to(array, (lax.axis_size(axis), *array.shape))
    return lax.all_to_all(copies, axis, split_axis=0, concat_axis=0, tiled=True)


def all_in_one(array, axis):
    leaves = jax.tree.leaves(array)
    order = sorted(range(len(leaves)), key=lambda k: -leaves[k].size)
    width = (1, *leaves[order[0]].shape)[-1]
    lines = [
        jnp.pad(leaves[k].reshape(-1), (0, -leaves[k].size % width)).reshape(-1, width)
        for k in order
    ]
    both, at, found = (copy_for_each(jnp.concatenate(lines), axis), 0, {})
    for k, line in zip(order, lines):
        section = both[:, at : at + len(line)].reshape(len(both), -1)
        found[k] = section[:, : leaves[k].size].reshape(-1, *leaves[k].shape)
        at += len(line)
    numbers = iter(range(len(leaves)))
    return jax.tree.map(lambda _: found[next(numbers)], array)


def joined_by_halves(pieces, combine):
    while len(jax.tree.leaves(pieces)[0]) > 1:
        pieces = jax.vmap(combine)(
            *(jax.tree.map(lambda part: part[side::2], pieces) for side in (0, 1))
        )
    return jax.tree.map(lambda part: part[0], pieces)


def merged_2(array, axis, combine):
    pieces = all_in_one(array, axis)
    return joined_by_halves(pieces, combine)


def over_copies(array, axis):
    return copy_for_each(array, axis).sum(axis=0)


def laid_out(blocks, dim):
    dims = list(blocks.shape[1:])
    dims[dim] *= blocks.shape[0]
    return jnp.moveaxis(blocks, 0, dim).reshape(dims)


def collect(array, axis, dim):
    blocks = copy_for_each(array, axis)
    return laid_out(blocks, dim)


def to_global(local, frames):
    rotation = frames[:9].reshape(3, 3, -1)
    moved = jnp.einsum("abn,ngb->nga", rotation, local, precision=HIGH)
    return moved + jnp.transpose(frames[9:12])[:, None, :]


def to_local(points, frames):
    rotation = frames[:9].reshape(3, 3, -1)
    moved = points - jnp.transpose(frames[9:12])[:, None, None, :]
    return jnp.einsum("abn,nhpa->nhpb", rotation, moved, precision=HIGH)


def compose(frames, motion):
    rotation = frames[:9].reshape(3, 3, -1)
    inverse = 1.0 / jnp.sqrt(1.0 + motion[:, 0] ** 2 + motion[:, 1] ** 2 + motion[:, 2] ** 2)
    quat_b = motion[:, 0] * inverse
    quat_c = motion[:, 1] * inverse
    quat_d = motion[:, 2] * inverse
    spin = jnp.stack(
        [
            inverse * inverse + quat_b * quat_b - quat_c * quat_c - quat_d * quat_d,
            2.0 * (quat_b * quat_c - inverse * quat_d),
            2.0 * (quat_b * quat_d + inverse * quat_c),
            2.0 * (quat_b * quat_c + inverse * quat_d),
            inverse * inverse - quat_b * quat_b + quat_c * quat_c - quat_d * quat_d,
            2.0 * (quat_c * quat_d - inverse * quat_b),
            2.0 * (quat_b * quat_d - inverse * quat_c),
            2.0 * (quat_c * quat_d + inverse * quat_b),
            inverse * inverse - quat_b * quat_b - quat_c * quat_c + quat_d * quat_d,
        ]
    ).reshape(3, 3, -1)
    new_rotation = jnp.einsum("abn,bcn->acn", rotation, spin, precision=HIGH)
    offset = jnp.einsum("abn,nb->an", rotation, motion[:, 3:6], precision=HIGH)
    return jnp.concatenate([new_rotation.reshape(9, -1), frames[9:12] + offset], axis=0)


def attention_logits(
    pair_rows,
    query_rows,
    query_points,
    query_chain,
    query_present,
    keys,
    key_points,
    key_chain,
    key_present,
    w_pair_bias,
    distance_scale,
    chain_bias,
):
    count_q = pair_rows.shape[0]
    count_k = pair_rows.shape[1]
    bias = jnp.dot(
        pair_rows.reshape(count_q * count_k, -1), w_pair_bias, preferred_element_type=jnp.float32
    ).reshape(count_q, count_k, -1)
    dots = jnp.einsum("ihc,jhc->ijh", query_rows, keys, precision=HIGH) / math.sqrt(keys.shape[-1])
    gaps = query_points[:, None] - key_points[None]
    distance = jnp.sum(gaps * gaps, axis=(3, 4))
    differ = (query_chain[:, None] != key_chain[None, :]).astype(jnp.float32)
    logits = LOGIT_WEIGHT * (
        dots + bias - distance_scale * distance + chain_bias * differ[..., None]
    )
    absent = 1.0 - query_present[:, None] * key_present[None, :]
    return logits - MASK_PENALTY * absent[..., None]


def rescale(values, factor):
    return values * factor.reshape(factor.shape + (1,) * (values.ndim - factor.ndim))


def fold_pair(first, second):
    best = jnp.maximum(first[0], second[0])
    first_scale = jnp.exp(first[0] - best)
    second_scale = jnp.exp(second[0] - best)
    merged = [
        rescale(left_part, first_scale) + rescale(right_part, second_scale)
        for left_part, right_part in zip(first[1:], second[1:])
    ]
    return (best,) + tuple(merged)


def body(
    single,
    pair,
    frames,
    chain,
    mask,
    w_query,
    w_key_value,
    w_query_points,
    w_kv_points,
    w_pair_bias,
    head_weights,
    chain_bias,
    w_out,
    out_gain,
    w_backbone,
):
    rows = single.shape[0]
    half = pair.shape[2]
    width = pair.shape[3]
    heads_here = w_pair_bias.shape[1]
    head_size = w_query.shape[1] // heads_here
    query_count = w_query_points.shape[1] // (3 * heads_here)
    value_count = w_kv_points.shape[1] // (3 * heads_here) - query_count
    pair_keys = pair.reshape(rows, pair.shape[1] * half, width)
    query = jnp.dot(single, w_query, preferred_element_type=jnp.float32).reshape(
        rows, heads_here, head_size
    )
    query_local = jnp.dot(single, w_query_points, preferred_element_type=jnp.float32)
    query_points = to_global(query_local.reshape(rows, heads_here * query_count, 3), frames)
    query_points = query_points.reshape(rows, heads_here, query_count, 3)
    query_chain = chain.astype(jnp.float32)
    query_present = mask.astype(jnp.float32)
    distance_scale = jax.nn.softplus(head_weights) * math.sqrt(2.0 / (9.0 * query_count)) / 2.0
    position = lax.axis_index("pair")
    key_single = lax.dynamic_slice_in_dim(single, position * half, half, 0)
    key_frames = lax.dynamic_slice_in_dim(frames, position * half, half, 1)
    key_chain = lax.dynamic_slice_in_dim(query_chain, position * half, half, 0)
    key_present = lax.dynamic_slice_in_dim(query_present, position * half, half, 0)
    key_value = jnp.dot(key_single, w_key_value, preferred_element_type=jnp.float32)
    key_local = jnp.dot(key_single, w_kv_points, preferred_element_type=jnp.float32)
    key_global = to_global(
        key_local.reshape(half, heads_here * (query_count + value_count), 3), key_frames
    )
    payload = jnp.concatenate([key_value, key_global.reshape(half, -1)], axis=1)
    key_meta = jnp.stack([key_chain, key_present], axis=1)
    split_at = heads_here * 2 * head_size
    pieces = side_by_side((payload, key_meta), "blk", 0, 1)
    moving = pieces[0]
    moving_meta = pieces[1]
    top = jnp.full((rows, heads_here), -1e30, jnp.float32)
    count = moving.shape[0]
    absorb_pieces = moving[:, :split_at].reshape(count, heads_here, 2, head_size)
    points = moving[:, split_at:].reshape(count, heads_here, query_count + value_count, 3)
    logits = attention_logits(
        pair_keys,
        query,
        query_points,
        query_chain,
        query_present,
        absorb_pieces[:, :, 0],
        points[:, :, :query_count],
        moving_meta[:, 0],
        moving_meta[:, 1],
        w_pair_bias,
        distance_scale,
        chain_bias,
    )
    new_top = jnp.maximum(top, jnp.max(logits, axis=1))
    weights = jnp.exp(logits - new_top[:, None, :])
    total = jnp.sum(weights, axis=1)
    sum_values = jnp.einsum("ijh,jhc->ihc", weights, absorb_pieces[:, :, 1], precision=HIGH)
    sum_points = jnp.einsum("ijh,jhpd->ihpd", weights, points[:, :, query_count:], precision=HIGH)
    sum_pair = jnp.einsum(
        "ijh,ijc->ihc", weights.astype(jnp.bfloat16), pair_keys, preferred_element_type=jnp.float32
    )
    carry = (new_top, total, sum_values, sum_points, sum_pair)
    best, total, sum_values, sum_points, sum_pair = merged_2(carry, "pair", fold_pair)
    attended = sum_values / total[..., None]
    pointed = to_local(sum_points / total[..., None, None], frames)
    point_norms = jnp.sqrt(jnp.sum(pointed * pointed, axis=3) + 1.0)
    paired = sum_pair / total[..., None]
    joined = jnp.concatenate(
        [attended, pointed.reshape(rows, heads_here, value_count * 3), point_norms, paired], axis=2
    ).astype(jnp.bfloat16)
    partial_update = jnp.dot(
        joined.reshape(rows, -1),
        w_out.reshape(-1, w_out.shape[2]),
        preferred_element_type=jnp.float32,
    )
    update = over_copies(partial_update, "head")
    mixed = single.astype(jnp.float32) + update
    centre = jnp.mean(mixed, axis=1, keepdims=True)
    spread = jnp.mean(jnp.square(mixed - centre), axis=1, keepdims=True)
    single_out = ((mixed - centre) * lax.rsqrt(spread + 1e-05) * out_gain).astype(jnp.bfloat16)
    motion = jnp.dot(single_out, w_backbone, preferred_element_type=jnp.float32)
    frames_new = compose(frames, motion)
    frames_out = collect(frames_new, "blk", 1)
    return (single_out, frames_out)


def solution(mesh):
    placed = (
        P(("groups", "blk"), None),
        P(("groups", "blk"), None, "pair", None),
        P(None, ("groups", "blk")),
        P(("groups", "blk")),
        P(("groups", "blk")),
        P(None, "head"),
        P(None, "head"),
        P(None, "head"),
        P(None, "head"),
        P(None, "head"),
        P("head"),
        P("head"),
        P("head", None, None),
        P(),
        P(),
    )
    return jax.shard_map(
        body,
        mesh=mesh,
        in_specs=placed,
        out_specs=(P(("groups", "blk"), None), P(None, "groups")),
        check_vma=False,
    )
```

profile of v0, /device:TPU:33, one launch (start us, length us, event | category | flops | bytes accessed | tf_op | source)
XLA Modules:
  0.0 168.2 jit_solution(1981582161542075526)
XLA Ops:
  0.7 0.8 slice_bitcast_fusion.4
  1.5 0.8 constant_dynamic-slice_fusion
  2.3 1.1 fusion.40
  3.3 0.1 copy.221
  3.5 0.1 copy.222
  3.6 0.8 dynamic-slice_bitcast_fusion
  4.4 0.2 convolution_add_fusion.1
  4.7 0.1 copy.224
  4.9 0.7 convert_element_type.27
  5.6 0.7 convert_element_type.28
  6.5 1.0 fusion.42
  7.6 84.4 %all_gather.3 = f32[512,206]{1,0:T(8,128)S(1)} all-gather(f32[16,206]{1,0:T(8,128)S(1)} %pad_maximum_fusion), channel_id=1, replica_groups=mesh['groups'=2,'blk'=32,'head'=4,'pair'=2] {'blk'}, dimensions={0}, use_global_device_ids=true | all-gather | bytes 435072 | tf_op jit(solution)/shard_map/all_gather | solution.py:16
  92.0 0.1 slice.190
  92.1 0.4 slice_reduce_fusion.1
  92.5 0.1 copy.238
  92.7 0.1 reshape.656
  92.9 0.1 copy.234
  93.1 0.1 fusion.64
  93.2 0.1 copy.233
  93.3 0.3 convolution_add_fusion
  93.7 0.1 copy.277
  93.9 0.1 copy.281
  94.1 0.1 fusion.63
  94.2 0.3 multiply_reduce_fusion
  94.6 3.4 %fusion.44 = f32[32,512,3]{1,2,0:T(4,128)S(1)} fusion(bf16[32,512,128]{2,1,0:T(8,128)(2,1)} %bitcast.174, bf16[128,3]{0,1:T(4,128)(2,1)S(1)} %copy-done.8), kind=kOutput, calls=%fused_computation.78 | convolution fusion | flops 12582912 | bytes 4391680 | tf_op jit(solution)/shard_map/dot_general | solution.py:122
  97.9 0.5 fusion.62
  98.5 0.4 convolution_bitcast_fusion.3
  98.8 0.2 fusion.20
  99.2 0.1 reshape.659
  99.3 0.4 convolution_bitcast_fusion.2
  99.7 0.2 copy.241
  99.9 0.2 reshape.658
  100.2 2.8 %fusion.18 = f32[32,3,128]{2,1,0:T(4,128)S(1)} fusion(bf16[32,512,128]{2,1,0:T(8,128)(2,1)} %bitcast.175, bf16[32,512,3]{1,0,2:T(8,128)(2,1)S(1)} %get-tuple-element.14), kind=kOutput, calls=%fused_computation.30 | convolution fusion | flops 12582912 | bytes 4341760 | tf_op jit(solution)/shard_map/ijh,ijc->ihc/dot_general | solution.py:224
  103.2 0.1 reshape.661
  103.3 0.1 max_broadcast_in_dim.12
  103.4 0.1 concatenate.14
  103.6 17.9 %all_to_all.15 = f32[2,128,128]{2,1,0:T(8,128)S(1)} all-to-all(f32[2,128,128]{2,1,0:T(8,128)S(1)} %broadcast_in_dim.9), channel_id=1, replica_groups=mesh['groups'=2,'blk'=32,'head'=4,'pair'=2] {'pair'}, dimensions={0} | all-to-all | bytes 262144 | tf_op jit(solution)/shard_map/all_to_all | solution.py:22
  121.5 0.1 slice.166
  121.6 0.1 slice.168
  121.8 0.1 slice.173
  121.9 0.1 slice.175
  122.2 0.1 slice.163
  122.5 0.3 slice.177
  122.7 0.3 slice.179
  123.0 0.1 copy.272
  123.1 3.9 %fusion.57 = (bf16[32,3,8,3]{2,3,1,0:T(4,128)(2,1)S(1)}, f32[32,3,8]{2,1,0:T(4,128)S(1)}) fusion(f32[3,3,32,1]{0,1,3,2:T(4,128)S(1)} %copy.272, f32[32,3,8,3]{3,2,1,0:T(8,128)S(1)} %slice.179, f32[32,3,8,3]{3,2,1,0:T(8,128)S(1)} %slice.177, f32[32,3]{1,0:T(8,128)S(1)} %copy.235, f32[32,3]{1,0:T(8,128)S(1)} %get-tuple-element.10, ...), kind=kOutput, calls=%fused_computation.116 | convolution fusion | flops 100608 | bytes 28800 | tf_op jit(solution)/shard_map/abn,nhpa->nhpb/dot_general | solution.py:79
  127.0 0.1 copy.254
  127.4 0.1 copy.262
  127.6 0.1 fusion.35
  127.7 0.1 fusion.36
  127.8 0.3 convolution_bitcast_fusion.1
  128.1 9.4 %all_to_all.16 = f32[4,32,384]{2,1,0:T(8,128)S(1)} all-to-all(f32[4,32,384]{2,1,0:T(8,128)S(1)} %broadcast_in_dim.10), channel_id=1, replica_groups=mesh['groups'=2,'blk'=32,'head'=4,'pair'=2] {'head'}, dimensions={0} | all-to-all | bytes 393216 | tf_op jit(solution)/shard_map/all_to_all | solution.py:22
  137.5 0.1 fusion.37
  137.7 0.2 multiply_reduce_fusion.2
  138.0 0.1 fusion.65
  138.2 0.1 copy.263
  138.3 0.3 convolution_bitcast_fusion
  138.7 0.1 copy.265
  138.9 0.1 reshape.699
  139.0 27.0 %all_to_all.17 = f32[32,1,384]{2,1,0:T(1,128)S(1)} all-to-all(f32[32,1,384]{2,1,0:T(1,128)S(1)} %reshape.699), channel_id=1, replica_groups=mesh['groups'=2,'blk'=32,'head'=4,'pair'=2] {'blk'}, dimensions={0} | all-to-all | bytes 98304 | tf_op jit(solution)/shard_map/all_to_all | solution.py:22
  166.0 0.5 broadcast.233
  166.5 0.8 reduce.22
  167.3 0.1 reshape.700
  167.5 0.8 reshape.668
  (82 shorter events, 2.3 us)
Async XLA Ops:
  0.6 127.2 %copy-start = (bf16[3,176,384]{2,1,0:T(8,128)(2,1)S(1)}, bf16[3,176,384]{2,1,0:T(8,128)(2,1)}, u32[]{:S(2)}) copy-start(bf16[3,176,384]{2,1,0:T(8,128)(2,1)} %param.27) | copy-start | bytes 1216516
  0.6 92.2 %copy-start.3 = (f32[12,32]{1,0:T(8,128)S(1)}, f32[12,32]{1,0:T(8,128)}, u32[]{:S(2)}) copy-start(f32[12,32]{1,0:T(8,128)} %param.17) | copy-start | bytes 4612
  0.7 92.4 %copy-start.1 = (bf16[32,384]{1,0:T(8,128)(2,1)S(1)}, bf16[32,384]{1,0:T(8,128)(2,1)}, u32[]{:S(2)}) copy-start(bf16[32,384]{1,0:T(8,128)(2,1)} %param.15) | copy-start | bytes 73732
  0.7 92.4 %copy-start.5 = (bf16[384,36]{0,1:T(8,128)(2,1)S(1)}, bf16[384,36]{0,1:T(8,128)(2,1)}, u32[]{:S(2)}) copy-start(bf16[384,36]{0,1:T(8,128)(2,1)} %param.22) | copy-start | bytes 82948
  0.7 93.4 %copy-start.4 = (bf16[384,48]{0,1:T(8,128)(2,1)S(1)}, bf16[384,48]{0,1:T(8,128)(2,1)}, u32[]{:S(2)}) copy-start(bf16[384,48]{0,1:T(8,128)(2,1)} %param.20) | copy-start | bytes 110596
  0.7 93.5 %copy-start.10 = (f32[3]{0:T(128)S(1)}, f32[3]{0:T(128)}, u32[]{:S(2)}) copy-start(f32[3]{0:T(128)} %param.25) | copy-start | bytes 40
  0.7 93.9 %copy-start.8 = (bf16[128,3]{0,1:T(4,128)(2,1)S(1)}, bf16[128,3]{0,1:T(4,128)(2,1)}, u32[]{:S(2)}) copy-start(bf16[128,3]{0,1:T(4,128)(2,1)} %param.24) | copy-start | bytes 2308
  92.5 5.5 %copy-start.9 = (f32[3]{0:T(128)S(1)}, f32[3]{0:T(128)}, u32[]{:S(2)}) copy-start(f32[3]{0:T(128)} %param.26) | copy-start | bytes 40
  103.0 34.8 %copy-start.7 = (f32[384]{0:T(512)S(1)}, f32[384]{0:T(512)}, u32[]{:S(2)}) copy-start(f32[384]{0:T(512)} %param.28) | copy-start | bytes 4612
  103.0 34.9 %copy-start.6 = (bf16[384,6]{0,1:T(8,128)(2,1)S(1)}, bf16[384,6]{0,1:T(8,128)(2,1)}, u32[]{:S(2)}) copy-start(bf16[384,6]{0,1:T(8,128)(2,1)} %param.29) | copy-start | bytes 13828
  138.0 30.3 %copy-start.2 = (bf16[32,384]{1,0:T(8,128)(2,1)}, bf16[32,384]{1,0:T(8,128)(2,1)S(1)}, u32[]{:S(2)}) copy-start(bf16[32,384]{1,0:T(8,128)(2,1)S(1)} %multiply_convert_fusion) | copy-start | bytes 73732
where the time goes:
time: 170 us; the launch traced here: 168 us
  blocking collectives  139 us (82%)
  matrix products  15.1 us (9%)
  local copies, waits for them, and re-layouts  9.68 us (6%)
  other arithmetic  3.57 us (2%)
    all_gather x1, blocking collectives, side_by_side(): out = lax.all_gather(both, axis, axis=dim, tiled=True)  84.4 us
    all_to_all x3, blocking collectives, copy_for_each(): return lax.all_to_all(copies, axis, split_axis=0, concat_axis=0, tiled=True)  54.3 us
    dot_general x1, matrix products, to_local(): return jnp.einsum('abn,nhpa->nhpb', rotation, moved, precision=HIGH)  3.88 us

commit v1 on v0

v1 whole, which is shorter than its diff:
```python
import functools
import math

import jax
import jax.numpy as jnp
import numpy as np
from jax import lax
from jax.experimental import pallas as pl
from jax.experimental.pallas import tpu as pltpu
from jax.sharding import PartitionSpec as P

MESH = pl.DeviceIdType.MESH
HIGH = lax.Precision.HIGHEST
F32 = jnp.float32
BF16 = jnp.bfloat16
LW = math.sqrt(1.0 / 3.0)
MASK_PENALTY = 100000.0
LANES = 128
SUB = 8
NT = (((1,), (1,)), ((), ()))

CHAIN_LANE = 7
MASK_LANE = 15
ONE_LANE = 120
TOP_LANE = 121


def gather_plan(n, stride, fixed, hop, weight):
    low, high = -((n - 1) // 2), n // 2
    when, parent = {0: 0.0}, {}
    anchors = [0]
    for sign in (1, -1):
        for k in range(1, n):
            o = sign * k * stride
            if not (low <= o <= high) or abs(o) > n // 2 - 2:
                break
            anchors.append(o)
            parent[o] = (o - sign * stride, sign * stride)
            when[o] = when[o - sign * stride] + fixed + hop * stride
    for o in range(low, high + 1):
        if o in when:
            continue
        best = min(
            anchors,
            key=lambda a: (when[a] + fixed + (hop + weight) * abs(o - a), abs(a)),
        )
        parent[o] = (best, o - best)
        when[o] = when[best] + fixed + hop * abs(o - best)
    order = sorted(when, key=lambda o: (when[o], abs(o), o))
    children = {}
    for o, (p, delta) in parent.items():
        children.setdefault(p, []).append((o, delta))
    for p in children:
        children[p].sort(key=lambda c: (c[0] not in anchors, -abs(c[1])))
    return order, children


def constants(heads, ch, pq, pv):
    key_lane = lambda h, c: ((h * ch + c) // 4) * 8 + 3 + (h * ch + c) % 4
    kp_lane = lambda h, p, a: (p * 3 + a) * 8 + h
    v_lane = lambda h, c: h * ch + c
    vp_lane = lambda h, p, a: heads * ch + a * heads * pv + h * pv + p
    kv = np.zeros((heads * 2 * ch, 2 * LANES), np.float32)
    kp = np.zeros((heads * (pq + pv) * 3, 6 * LANES), np.float32)
    fr = np.zeros((16, 8 * LANES), np.float32)
    q = np.zeros((heads * ch, LANES), np.float32)
    qp = np.zeros((heads * pq * 3, 3 * LANES), np.float32)
    pa = np.zeros((LANES, LANES), np.float32)
    masks = np.zeros((3, SUB, LANES), np.float32)
    perm = np.zeros((2 * LANES, heads * (ch + 4 * pv)), np.float32)
    small = ch + 4 * pv
    for h in range(heads):
        for c in range(ch):
            kv[h * 2 * ch + c, key_lane(h, c)] = 1
            kv[h * 2 * ch + ch + c, LANES + v_lane(h, c)] = 1
            q[h * ch + c, key_lane(h, c)] = 1
            masks[0, h, key_lane(h, c)] = 1
            masks[2, h, v_lane(h, c)] = 1
            perm[v_lane(h, c), h * small + c] = 1
        for p in range(pq):
            for a in range(3):
                lane = kp_lane(h, p, a)
                masks[1, h, lane] = 1
                pa[lane, p * 3 + a] = 1
                for b in range(3):
                    kp[(h * (pq + pv) + p) * 3 + b, 2 * b * LANES + lane] = 1
                    qp[(h * pq + p) * 3 + b, b * LANES + lane] = 1
                    fr[3 * a + b, 2 * b * LANES + lane] = 1
                fr[9 + a, 6 * LANES + lane] = 1
        for p in range(pv):
            for a in range(3):
                lane = vp_lane(h, p, a)
                masks[2, h, lane] = 1
                perm[lane, h * small + ch + p * 3 + a] = 1
                for b in range(3):
                    kp[(h * (pq + pv) + pq + p) * 3 + b, (2 * b + 1) * LANES + lane] = 1
                    fr[3 * a + b, (2 * b + 1) * LANES + lane] = 1
                fr[9 + a, 7 * LANES + lane] = 1
            perm[LANES + vp_lane(h, p, 0), h * small + ch + 3 * pv + p] = 1
    masks[1, :heads, CHAIN_LANE] = 1
    masks[1, :heads, MASK_LANE] = 1
    pa[CHAIN_LANE, 12] = 1
    pa[MASK_LANE, 13] = 1
    fr[12, 6 * LANES + CHAIN_LANE] = 1
    fr[13, 6 * LANES + MASK_LANE] = 1
    fr[14, 7 * LANES + ONE_LANE] = 1
    return (kv, kp, fr, q, qp, pa, perm), masks.reshape(3 * SUB, LANES)


def pieces3(x):
    a = x.astype(BF16)
    r = x - a.astype(F32)
    b = r.astype(BF16)
    c = (r - b.astype(F32)).astype(BF16)
    return a, b, c


def select(x, onehot):
    m = x.shape[0]
    y = jnp.dot(jnp.concatenate(pieces3(x), axis=0), onehot, preferred_element_type=F32)
    return y[:m] + y[m : 2 * m] + y[2 * m :]


def roll(x, shift, axis):
    shift %= x.shape[axis]
    return x if shift == 0 else pltpu.roll(x, shift, axis)


def kernel(
    cfg,
    single,
    pair,
    frames,
    chain,
    mask,
    w_q,
    w_kv,
    w_qp,
    w_kvp,
    w_pb,
    head_w,
    chain_b,
    w_out,
    gain,
    w_bb,
    c_kv,
    c_kp,
    c_fr,
    c_q,
    c_qp,
    c_pa,
    c_perm,
    c_masks,
    out_single,
    out_frames,
    pv,
    buf,
    stack,
    ft,
    bias,
    qpb,
    qblk,
    kt,
    dots,
    wts,
    alpha,
    acc,
    mbuf,
    xbuf,
    fbuf,
    sbuf,
    wp,
    rb,
    rsel,
    pair_sem,
    send_sem,
    recv_sem,
    m_sem,
    x_send,
    x_recv,
    s_sem,
    f_send,
    f_recv,
):
    n, nx, heads, ch, pq, nv, half, chunk, order, children, deltas = cfg
    rows = 2 * half
    z = lax.axis_index("blk")
    x = lax.axis_index("head")
    p = lax.axis_index("pair")
    other = 1 - p
    slot_of = {o: i for i, o in enumerate(order)}

    def block(o):
        return lax.rem(z - o + 2 * n, n)

    pair_copies = []
    for o in order:
        copy = pltpu.make_async_copy(
            pair.at[:, block(o)], pv.at[:, slot_of[o]], pair_sem.at[slot_of[o]]
        )
        copy.start()
        pair_copies.append(copy)

    barrier = pltpu.get_barrier_semaphore()
    signals = 0
    for d in deltas:
        pl.semaphore_signal(
            barrier, inc=1, device_id={"blk": lax.rem(z + d + n, n)}, device_id_type=MESH
        )
        signals += 1
    for d in range(1, nx):
        pl.semaphore_signal(
            barrier, inc=1, device_id={"head": lax.rem(x + d, nx)}, device_id_type=MESH
        )
        signals += 1
    pl.semaphore_signal(barrier, inc=1, device_id={"pair": other}, device_id_type=MESH)
    signals += 1

    stack[...] = jnp.zeros_like(stack)
    stack[0:12, :] = frames[...]
    stack[12:13, :] = chain[...].astype(F32)
    stack[13:14, :] = mask[...].astype(F32)
    stack[14:15, :] = jnp.ones((1, rows), F32)
    eye = (
        lax.broadcasted_iota(jnp.int32, (rows, rows), 0)
        == lax.broadcasted_iota(jnp.int32, (rows, rows), 1)
    ).astype(F32)
    ft[...] = lax.dot_general(eye, stack[...], NT, precision=HIGH, preferred_element_type=F32)
    mine = pl.ds(pl.multiple_of(p * half, half), half)
    theirs = pl.ds(pl.multiple_of(other * half, half), half)
    ks = single[mine, :]
    key_value = jnp.dot(ks, w_kv[...], preferred_element_type=F32)
    key_local = jnp.dot(ks, w_kvp[...], preferred_element_type=F32)
    turn = select(ft[mine, :], c_fr[...])
    local = select(key_local, c_kp[...])
    width = 2 * LANES
    line = select(key_value, c_kv[...]) + turn[:, 3 * width :]
    for b in range(3):
        line += turn[:, b * width : (b + 1) * width] * local[:, b * width : (b + 1) * width]
    buf[0, 0] = line[:, :LANES]
    buf[0, 1] = line[:, LANES:]

    sends = []

    def relay(o):
        for child, delta in children.get(o, []):
            copy = pltpu.make_async_remote_copy(
                src_ref=buf.at[slot_of[o]],
                dst_ref=buf.at[slot_of[child]],
                send_sem=send_sem.at[slot_of[child]],
                recv_sem=recv_sem.at[slot_of[child]],
                device_id={"blk": lax.rem(z + delta + n, n)},
                device_id_type=MESH,
            )
            copy.start()
            sends.append(copy)

    arrived = set()

    def arrive(o):
        if o == 0 or o in arrived:
            return
        arrived.add(o)
        pltpu.make_async_remote_copy(
            src_ref=buf.at[slot_of[o]],
            dst_ref=buf.at[slot_of[o]],
            send_sem=send_sem.at[slot_of[o]],
            recv_sem=recv_sem.at[slot_of[o]],
            device_id={"blk": lax.rem(z + 1, n)},
            device_id_type=MESH,
        ).wait_recv()
        relay(o)

    pl.semaphore_wait(barrier, signals)
    relay(0)

    full = ft[...]
    query = jnp.dot(single[...], w_q[...], preferred_element_type=F32)
    query = select(query, c_q[...]) * (LW / math.sqrt(ch))
    q_local = select(jnp.dot(single[...], w_qp[...], preferred_element_type=F32), c_qp[...])
    q_turn = select(full, c_fr[...])
    q_line = q_turn[:, 3 * width : 3 * width + LANES]
    for b in range(3):
        q_line += (
            q_turn[:, b * width : b * width + LANES] * q_local[:, b * LANES : (b + 1) * LANES]
        )
    head_keys = c_masks[0:SUB, :]
    head_points = c_masks[SUB : 2 * SUB, :]
    head_values = c_masks[2 * SUB : 3 * SUB, :]
    qblk[...] = (query[:, None, :] * head_keys[None]).reshape(rows * SUB, LANES)
    spread = select((q_line[:, None, :] * head_points[None]).reshape(rows * SUB, LANES), c_pa[...])
    spread = spread.reshape(rows, SUB, LANES)
    marks = 3 * pq + 2
    for k in range(marks):
        qpb[:, k] = jnp.broadcast_to(spread[:, :, k : k + 1], (rows, SUB, LANES))

    head_row = lax.broadcasted_iota(jnp.int32, (SUB, LANES), 0)
    raw = jnp.zeros((SUB, LANES), F32)
    cross = jnp.zeros((SUB, LANES), F32)
    for h in range(heads):
        raw = jnp.where(head_row == h, head_w[h], raw)
        cross = jnp.where(head_row == h, chain_b[h] * LW, cross)
    soft = jnp.maximum(raw, 0.0) + jnp.log1p(jnp.exp(-jnp.abs(raw)))
    near = soft * (LW * math.sqrt(2.0 / (9.0 * pq)) / 2.0)

    eye_h = (
        lax.broadcasted_iota(jnp.int32, (SUB, heads), 0)
        == lax.broadcasted_iota(jnp.int32, (SUB, heads), 1)
    ).astype(BF16)
    w_bias = lax.dot_general(eye_h, w_pb[...], NT, preferred_element_type=F32).astype(BF16)

    for copy in pair_copies:
        copy.wait()

    keys = n * half

    def bias_of(i, _):
        bias[i] = LW * lax.dot_general(
            w_bias, pv[i].reshape(keys, LANES), NT, preferred_element_type=F32
        )
        return 0

    events = [o for o in order if children.get(o) and o != 0]
    lax.fori_loop(0, rows, bias_of, 0, unroll=4)

    short = w_out.shape[1] - LANES
    w_short = w_out[:, 0:short, :].reshape(heads * short, w_out.shape[2])
    wp[...] = jnp.dot(c_perm[...], w_short, preferred_element_type=F32).astype(BF16)
    mine_ft = ft[mine, :]
    for k in range(12):
        rb[k] = jnp.broadcast_to(mine_ft[:, k : k + 1], (half, LANES))
    lane = lax.broadcasted_iota(jnp.int32, (rows, LANES), 1)
    repeat = ((lane & (half - 1)) + p * half == lax.broadcasted_iota(jnp.int32, (rows, LANES), 0)).astype(BF16)
    wide = select(stack[...], repeat)
    lane8 = lax.broadcasted_iota(jnp.int32, (SUB, LANES), 1)
    part8 = lax.div(lane8, half)
    comp8 = lax.broadcasted_iota(jnp.int32, (SUB, LANES), 0) * (LANES // half) + part8
    for b in range(4):
        picked = jnp.zeros((SUB, LANES), F32)
        for k in range(12):
            source = (k - k % 3 + b if k < 9 else 3 * (k - 9) + b) if b < 3 else k
            if b == 3 and k < 9:
                continue
            picked = jnp.where(comp8 == k, wide[source : source + 1, :], picked)
        rsel[b] = picked
    eye_b = (
        lax.broadcasted_iota(jnp.int32, (SUB, w_bb.shape[1]), 0)
        == lax.broadcasted_iota(jnp.int32, (SUB, w_bb.shape[1]), 1)
    ).astype(BF16)
    w_motion = lax.dot_general(eye_b, w_bb[...], NT, preferred_element_type=F32).astype(BF16)

    span = chunk * half
    acc[...] = jnp.zeros_like(acc)
    alpha[...] = jnp.full(alpha.shape, -1e30, F32)
    for c in range(n // chunk):
        slots = slice(c * chunk, (c + 1) * chunk)
        for o in order[slots]:
            arrive(o)
        if c + 1 < n // chunk:
            pass
        kc = buf[slots, 0].reshape(span, LANES)
        vc = buf[slots, 1].reshape(span, LANES)
        kt[...] = kc.T.reshape(LANES // SUB, SUB, span)
        dots[...] = lax.dot_general(
            qblk[...], kc, NT, precision=HIGH, preferred_element_type=F32
        ).reshape(rows, SUB, span)
        chain_j = kt[0, 7:8, :]
        mask_j = kt[1, 7:8, :]

        def one_row(i, _):
            far = jnp.zeros((SUB, span), F32)
            for k in range(3 * pq):
                gap = qpb[i, k][:, :span] - kt[k]
                far += gap * gap
            differ = jnp.where(qpb[i, 3 * pq][:, :span] != chain_j, cross[:, :span], 0.0)
            absent = 1.0 - qpb[i, 3 * pq + 1][:, :span] * mask_j
            logits = (
                dots[i]
                + bias[i, :, c * span : (c + 1) * span]
                - near[:, :span] * far
                + differ
                - MASK_PENALTY * absent
            )
            old = alpha[i]
            top = jnp.maximum(old, jnp.max(logits, axis=1, keepdims=True))
            w = jnp.exp(logits - top[:, :span])
            wts[i] = w
            alpha[i] = top
            scale = jnp.exp(old - top)
            acc[i, 1] = acc[i, 1] * scale
            acc[i, 0] = acc[i, 0] * scale + jnp.dot(
                w.astype(BF16),
                pv[i, slots].reshape(span, LANES),
                preferred_element_type=F32,
            )
            return 0

        lax.fori_loop(0, rows, one_row, 0, unroll=4)
        acc[:, 1] += jnp.dot(
            wts[...].reshape(rows * SUB, span), vc, precision=HIGH, preferred_element_type=F32
        ).reshape(rows, SUB, LANES)

    lane3 = lax.broadcasted_iota(jnp.int32, (rows, SUB, LANES), 2)
    acc[:, 1] = jnp.where(lane3 == TOP_LANE, alpha[...], acc[:, 1])
    give = pltpu.make_async_remote_copy(
        src_ref=acc.at[theirs],
        dst_ref=mbuf,
        send_sem=m_sem.at[0],
        recv_sem=m_sem.at[1],
        device_id={"pair": other},
        device_id_type=MESH,
    )
    give.start()
    give.wait_recv()
    own_p, own_b = acc[mine, 0], acc[mine, 1]
    far_p, far_b = mbuf[:, 0], mbuf[:, 1]
    own_top, far_top = own_b[:, :, TOP_LANE : TOP_LANE + 1], far_b[:, :, TOP_LANE : TOP_LANE + 1]
    top = jnp.maximum(own_top, far_top)
    own_scale, far_scale = jnp.exp(own_top - top), jnp.exp(far_top - top)
    both_b = own_b * own_scale + far_b * far_scale
    total = both_b[:, :, ONE_LANE : ONE_LANE + 1]
    both_b = both_b / total * head_values[None]
    paired = (own_p * own_scale + far_p * far_scale) / total
    mbuf[:, 0] = paired
    sums = jnp.sum(both_b, axis=1)
    first = heads * ch
    third = heads * nv
    moved = [roll(sums, -a * third, 1) - rb[9 + a] for a in range(3)]
    pointed = [sum(rb[3 * a + b] * moved[a] for a in range(3)) for b in range(3)]
    norms = jnp.sqrt(pointed[0] * pointed[0] + pointed[1] * pointed[1] + pointed[2] * pointed[2] + 1.0)
    lane16 = lax.broadcasted_iota(jnp.int32, (half, LANES), 1)
    joined = sums
    for b in range(3):
        joined = jnp.where(
            (lane16 >= first + b * third) & (lane16 < first + (b + 1) * third),
            roll(pointed[b], b * third, 1),
            joined,
        )
    norms = jnp.where((lane16 >= first) & (lane16 < first + third), norms, 0.0)
    features = jnp.concatenate([joined, norms], axis=1).astype(BF16)
    update = jnp.dot(features, wp[...], preferred_element_type=F32)
    for h in range(heads):
        update += jnp.dot(
            mbuf[:, 0, h, :].astype(BF16), w_out[h, short:, :], preferred_element_type=F32
        )

    xbuf[x] = update
    x_copies = []
    for d in range(1, nx):
        copy = pltpu.make_async_remote_copy(
            src_ref=xbuf.at[x],
            dst_ref=xbuf.at[x],
            send_sem=x_send.at[d - 1],
            recv_sem=x_recv.at[d - 1],
            device_id={"head": lax.rem(x + d, nx)},
            device_id_type=MESH,
        )
        copy.start()
        x_copies.append(copy)
    for d in range(1, nx):
        source = lax.rem(x - d + nx, nx)
        pltpu.make_async_remote_copy(
            src_ref=xbuf.at[source],
            dst_ref=xbuf.at[source],
            send_sem=x_send.at[d - 1],
            recv_sem=x_recv.at[d - 1],
            device_id={"head": source},
            device_id_type=MESH,
        ).wait_recv()
    update = xbuf[0]
    for k in range(1, nx):
        update = update + xbuf[k]
    mixed = single[mine, :].astype(F32) + update
    count = mixed.shape[1]
    centre = jnp.sum(mixed, axis=1, keepdims=True) * (1.0 / count)
    apart = mixed - centre
    variance = jnp.sum(apart * apart, axis=1, keepdims=True) * (1.0 / count)
    result = (apart * lax.rsqrt(variance + 1e-05) * gain[...]).astype(BF16)
    out_single[mine, :] = result
    sbuf[0] = result.astype(F32)
    give_s = pltpu.make_async_remote_copy(
        src_ref=sbuf.at[0],
        dst_ref=sbuf.at[1],
        send_sem=s_sem.at[0],
        recv_sem=s_sem.at[1],
        device_id={"pair": other},
        device_id_type=MESH,
    )

    groups = LANES // half
    motion = lax.dot_general(
        w_motion,
        jnp.concatenate([result] * groups, axis=0),
        NT,
        preferred_element_type=F32,
    )
    m = [jnp.broadcast_to(motion[k : k + 1, :], (SUB, LANES)) for k in range(6)]
    qa = 1.0 / jnp.sqrt(1.0 + m[0] * m[0] + m[1] * m[1] + m[2] * m[2])
    qb, qc, qd = m[0] * qa, m[1] * qa, m[2] * qa
    aa, bb, cc, dd = qa * qa, qb * qb, qc * qc, qd * qd
    ab, ac, ad = qa * qb, qa * qc, qa * qd
    bc, bd, cd = qb * qc, qb * qd, qc * qd
    spin = [
        [aa + bb - cc - dd, 2.0 * (bc - ad), 2.0 * (bd + ac)],
        [2.0 * (bc + ad), aa - bb + cc - dd, 2.0 * (cd - ab)],
        [2.0 * (bd - ac), 2.0 * (cd + ab), aa - bb - cc + dd],
    ]
    column = lax.rem(comp8, 3)
    packed = rsel[3]
    for b in range(3):
        value = jnp.where(column == 0, spin[b][0], jnp.where(column == 1, spin[b][1], spin[b][2]))
        value = jnp.where(comp8 < 9, value, m[3 + b])
        packed = packed + rsel[b] * value
    lines = fbuf.shape[1]
    me = z * 2 + p
    fbuf[me] = packed[0:lines, :]

    f_copies = []
    steps = sorted(
        ((d, c) for d in range(n) for c in (0, 1) if (d, c) != (0, 0)),
        key=lambda s: (-min(s[0], n - s[0]), s[1]),
    )
    for d, c in steps:
        device = {"blk": lax.rem(z + d, n), "pair": p if c == 0 else other}
        copy = pltpu.make_async_remote_copy(
            src_ref=fbuf.at[me],
            dst_ref=fbuf.at[me],
            send_sem=f_send.at[2 * d + c],
            recv_sem=f_recv.at[2 * d + c],
            device_id=device,
            device_id_type=MESH,
        )
        copy.start()
        f_copies.append(copy)
    give_s.start()
    give_s.wait_recv()
    out_single[theirs, :] = sbuf[1].astype(BF16)
    for d, c in reversed(steps):
        source = lax.rem(z - d + n, n) * 2 + (p if c == 0 else other)
        pltpu.make_async_remote_copy(
            src_ref=fbuf.at[source],
            dst_ref=fbuf.at[source],
            send_sem=f_send.at[2 * d + c],
            recv_sem=f_recv.at[2 * d + c],
            device_id={"pair": other},
            device_id_type=MESH,
        ).wait_recv()

    gap = (lax.broadcasted_iota(jnp.int32, (SUB, LANES), 0) - part8) & (SUB - 1)
    for t in range(2 * n // groups):
        for line_number in range(2):
            tile = fbuf[t * groups : (t + 1) * groups, line_number, :]
            out = tile
            for s in range(1, groups):
                out = jnp.where(gap == s, roll(roll(tile, s, 0), -half * s, 1), out)
            height = 8 if line_number == 0 else 4
            out_frames[8 * line_number : 8 * line_number + height, t * LANES : (t + 1) * LANES] = out[:height]

    for copy in sends + x_copies + f_copies:
        copy.wait_send()
    give.wait_send()
    give_s.wait_send()


def body(n, nx, *args):
    (
        single,
        pair,
        frames,
        chain,
        mask,
        w_q,
        w_kv,
        w_qp,
        w_kvp,
        w_pb,
        head_w,
        chain_b,
        w_out,
        gain,
        w_bb,
    ) = args
    rows, half = single.shape[0], pair.shape[2]
    heads = w_pb.shape[1]
    ch = w_q.shape[1] // heads
    pq = w_qp.shape[1] // (3 * heads)
    nv = w_kvp.shape[1] // (3 * heads) - pq
    order, children = gather_plan(n, 6 if n >= 16 else 2, 0.9, 0.72, 0.4)
    deltas = sorted({d for kids in children.values() for _, d in kids})
    deltas = sorted(set(deltas) | {-d for d in deltas})
    deltas = [d for i, d in enumerate(deltas) if d % n not in {e % n for e in deltas[:i]}]
    chunk = min(8, n)
    cfg = (n, nx, heads, ch, pq, nv, half, chunk, order, children, deltas)
    hots, masks = constants(heads, ch, pq, nv)
    hots = [jnp.asarray(h, BF16) for h in hots]
    masks = jnp.asarray(masks, F32)
    vmem = pl.BlockSpec(memory_space=pltpu.VMEM)
    smem = pl.BlockSpec(memory_space=pltpu.SMEM)
    hbm = pl.BlockSpec(memory_space=pl.ANY)
    specs = [vmem, hbm, vmem, vmem, vmem, vmem, vmem, vmem, vmem, vmem, smem, smem]
    specs += [vmem] * (3 + len(hots) + 1)
    marks = 3 * pq + 2
    span = chunk * half
    width = w_out.shape[2]
    scratch = [
        pltpu.VMEM((rows, n, half, LANES), BF16),
        pltpu.VMEM((n, 2, half, LANES), F32),
        pltpu.VMEM((16, rows), F32),
        pltpu.VMEM((rows, 16), F32),
        pltpu.VMEM((rows, SUB, n * half), F32),
        pltpu.VMEM((rows, marks, SUB, LANES), F32),
        pltpu.VMEM((rows * SUB, LANES), F32),
        pltpu.VMEM((LANES // SUB, SUB, span), F32),
        pltpu.VMEM((rows, SUB, span), F32),
        pltpu.VMEM((rows, SUB, span), F32),
        pltpu.VMEM((rows, SUB, LANES), F32),
        pltpu.VMEM((rows, 2, SUB, LANES), F32),
        pltpu.VMEM((half, 2, SUB, LANES), F32),
        pltpu.VMEM((nx, half, width), F32),
        pltpu.VMEM((2 * n, 2, LANES), F32),
        pltpu.VMEM((2, half, width), F32),
        pltpu.VMEM((2 * LANES, width), BF16),
        pltpu.VMEM((12, half, LANES), F32),
        pltpu.VMEM((4, SUB, LANES), F32),
        pltpu.SemaphoreType.DMA((n,)),
        pltpu.SemaphoreType.DMA((n,)),
        pltpu.SemaphoreType.DMA((n,)),
        pltpu.SemaphoreType.DMA((2,)),
        pltpu.SemaphoreType.DMA((max(nx - 1, 1),)),
        pltpu.SemaphoreType.DMA((max(nx - 1, 1),)),
        pltpu.SemaphoreType.DMA((2,)),
        pltpu.SemaphoreType.DMA((2 * n,)),
        pltpu.SemaphoreType.DMA((2 * n,)),
    ]
    return pl.pallas_call(
        functools.partial(kernel, cfg),
        out_shape=(
            jax.ShapeDtypeStruct(single.shape, BF16),
            jax.ShapeDtypeStruct((12, n * rows), F32),
        ),
        in_specs=specs,
        out_specs=(vmem, vmem),
        scratch_shapes=scratch,
        compiler_params=pltpu.CompilerParams(collective_id=0, has_side_effects=True),
        name="layer",
    )(
        single,
        pair,
        frames,
        chain.reshape(1, rows),
        mask.reshape(1, rows),
        w_q,
        w_kv,
        w_qp,
        w_kvp,
        w_pb,
        head_w,
        chain_b,
        w_out,
        gain.reshape(1, -1),
        w_bb,
        *hots,
        masks,
    )


def solution(mesh):
    placed = (
        P(("groups", "blk"), None),
        P(("groups", "blk"), None, "pair", None),
        P(None, ("groups", "blk")),
        P(("groups", "blk")),
        P(("groups", "blk")),
        P(None, "head"),
        P(None, "head"),
        P(None, "head"),
        P(None, "head"),
        P(None, "head"),
        P("head"),
        P("head"),
        P("head", None, None),
        P(),
        P(),
    )
    return jax.shard_map(
        functools.partial(body, mesh.shape["blk"], mesh.shape["head"]),
        mesh=mesh,
        in_specs=placed,
        out_specs=(P(("groups", "blk"), None), P(None, "groups")),
        check_vma=False,
    )
```

time: 170 us -> 120 us (0.71)
  blocking collectives: 139 us -> 0 us
  Pallas kernels: 0 us -> 105 us
  matrix products: 15.1 us -> 0 us
  other arithmetic: 3.57 us -> 0 us
  local copies, waits for them, and re-layouts: 9.68 us -> 13.2 us
    pallas_call x0 -> x1, Pallas kernels: none -> 105 us  [body(): pl.pallas_call(functools.partial(kernel, cfg), out_shape=(jax.ShapeDtypeS...]
    all_gather x1 -> x0, blocking collectives: 84.4 us -> none  [side_by_side(): out = lax.all_gather(both, axis, axis=dim, tiled=True)]
    all_to_all x3 -> x0, blocking collectives: 54.3 us -> none  [copy_for_each(): return lax.all_to_all(copies, axis, split_axis=0, concat_axis=0, tiled=True)]
    dot_general x15 -> x0, matrix products: 15.1 us -> none  [the longest x1 3.88 us: to_local(): return jnp.einsum('abn,nhpa->nhpb', rotation, moved, precision=HIGH)]
    unnamed x25 -> x8, local copies, waits for them, and re-layouts: 0.43 us -> 12 us
    slice x24 -> x0, local copies, waits for them, and re-layouts: 2.76 us -> none  [the longest x15 1.26 us: joined_by_halves(): part[side::2]]
    transpose x8 -> x0, local copies, waits for them, and re-layouts: 2.2 us -> none  [the longest x4 1.71 us: to_global(): return moved + jnp.transpose(frames[9:12])[:, None, :]]
where the time goes in v1:
time: 120 us; the launch traced here: 119 us
  Pallas kernels  105 us (88%)
  local copies, waits for them, and re-layouts  13.2 us (11%)
    pallas_call x1, Pallas kernels, body(): pl.pallas_call(functools.partial(kernel, cfg), out_shape=(jax.ShapeDtypeS...  105 us
    unnamed x8, local copies, waits for them, and re-layouts  12 us

profile of v1, /device:TPU:33, one launch (start us, length us, event | category | flops | bytes accessed | tf_op | source)
XLA Modules:
  0.0 119.0 jit_solution(14325666342498499460)
XLA Ops:
  0.6 1.2 %reshape.15.gain = f32[1,384]{1,0:T(1,128)} reshape(f32[384]{0:T(512)} %param.36) | data formatting | bytes 3072 | tf_op jit(solution)/shard_map/reshape | solution.py:660
  1.9 1.4 %copy.29.w_pb = bf16[128,3]{1,0:T(8,128)(2,1)} copy(bf16[128,3]{0,1:T(4,128)(2,1)} %param.32) | data formatting | bytes 1536 | tf_op args[9]
  3.3 1.5 %copy.25.w_q = bf16[384,48]{1,0:T(8,128)(2,1)} copy(bf16[384,48]{0,1:T(8,128)(2,1)} %param.28) | data formatting | bytes 73728 | tf_op args[5]
  4.8 1.6 %copy.26.w_kv = bf16[384,96]{1,0:T(8,128)(2,1)} copy(bf16[384,96]{0,1:T(8,128)(2,1)} %param.29) | data formatting | bytes 147456 | tf_op args[6]
  6.4 1.5 %copy.27.w_qp = bf16[384,36]{1,0:T(8,128)(2,1)} copy(bf16[384,36]{0,1:T(8,128)(2,1)} %param.30) | data formatting | bytes 55296 | tf_op args[7]
  7.9 1.6 %copy.28.w_kvp = bf16[384,108]{1,0:T(8,128)(2,1)} copy(bf16[384,108]{0,1:T(8,128)(2,1)} %param.31) | data formatting | bytes 165888 | tf_op args[8]
  9.6 1.5 %copy.30.w_bb = bf16[384,6]{1,0:T(8,128)(2,1)} copy(bf16[384,6]{0,1:T(8,128)(2,1)} %param.37) | data formatting | bytes 9216 | tf_op args[14]
  11.0 105.2 %layer.1 = (bf16[32,384]{1,0:T(8,128)(2,1)}, f32[12,1024]{1,0:T(8,128)}) custom-call(bf16[32,384]{1,0:T(8,128)(2,1)} %single.1, bf16[32,32,16,128]{3,2,1,0:T(8,128)(2,1)} %pair.1, f32[12,32]{1,0:T(8,128)} %frames.1, s32[1,32]{1,0:T(1,128)} %bitcast.2, s32[1,32]{1,0:T(1,128)} %bitcast.3, bf16[384,48]{1,0:T(8,128)(2,1)} %copy.25.w_q, ...), custom_call_target="tpu_custom_call" | custom-call | tf_op jit(solution)/shard_map/layer/pallas_call | solution.py:635
  116.2 1.3 %copy.33 = bf16[32,384]{1,0:T(8,128)(2,1)} copy(bf16[32,384]{1,0:T(8,128)(2,1)} %get-tuple-element.4) | data formatting | bytes 49152
  117.6 1.5 %copy.34 = f32[12,1024]{1,0:T(8,128)} copy(f32[12,1024]{1,0:T(8,128)} %get-tuple-element.5) | data formatting | bytes 98304

commit v2 on v1

--- a/solution.py
+++ b/solution.py
@@ -15,6 +15,7 @@
 BF16 = jnp.bfloat16
 LW = math.sqrt(1.0 / 3.0)
 MASK_PENALTY = 100000.0
+KEY_PATH = 9
 LANES = 128
 SUB = 8
 NT = (((1,), (1,)), ((), ()))
@@ -46,13 +47,14 @@
         )
         parent[o] = (best, o - best)
         when[o] = when[best] + fixed + hop * abs(o - best)
-    order = sorted(when, key=lambda o: (when[o], abs(o), o))
+    order = sorted(when, key=lambda o: (o not in anchors, when[o], abs(o), o))
+    anchors = [o for o in order if o in anchors]
     children = {}
     for o, (p, delta) in parent.items():
         children.setdefault(p, []).append((o, delta))
     for p in children:
         children[p].sort(key=lambda c: (c[0] not in anchors, -abs(c[1])))
-    return order, children
+    return order, anchors, children
 
 
 def constants(heads, ch, pq, pv):
@@ -128,31 +130,23 @@
 
 def kernel(
     cfg,
-    single,
     pair,
-    frames,
-    chain,
-    mask,
-    w_q,
-    w_kv,
-    w_qp,
-    w_kvp,
-    w_pb,
-    head_w,
-    chain_b,
-    w_out,
-    gain,
-    w_bb,
-    c_kv,
-    c_kp,
-    c_fr,
-    c_q,
-    c_qp,
-    c_pa,
-    c_perm,
-    c_masks,
+    *refs,
+):
+    n_loads = cfg[-1]
+    sources, (out_single, out_frames) = refs[:n_loads], refs[n_loads : n_loads + 2]
+    held = refs[n_loads + 2 : 2 * n_loads + 2]
+    run(cfg[:-1], pair, sources, held, out_single, out_frames, *refs[2 * n_loads + 2 :])
+
+
+def run(
+    cfg,
+    pair,
+    sources,
+    held,
     out_single,
     out_frames,
+    load_sem,
     pv,
     buf,
     stack,
@@ -176,13 +170,11 @@
     send_sem,
     recv_sem,
     m_sem,
-    x_send,
-    x_recv,
+    x_sem,
     s_sem,
-    f_send,
-    f_recv,
+    f_sem,
 ):
-    n, nx, heads, ch, pq, nv, half, chunk, order, children, deltas = cfg
+    n, nx, heads, ch, pq, nv, half, chunk, order, anchors, children, deltas = cfg
     rows = 2 * half
     z = lax.axis_index("blk")
     x = lax.axis_index("head")
@@ -190,16 +182,12 @@
     other = 1 - p
     slot_of = {o: i for i, o in enumerate(order)}
 
+    group_of = {o: i for i, o in enumerate(anchors)}
+    for i, o in enumerate(order[len(anchors) :], len(anchors)):
+        group_of[o] = len(anchors) + i // chunk
+
     def block(o):
         return lax.rem(z - o + 2 * n, n)
-
-    pair_copies = []
-    for o in order:
-        copy = pltpu.make_async_copy(
-            pair.at[:, block(o)], pv.at[:, slot_of[o]], pair_sem.at[slot_of[o]]
-        )
-        copy.start()
-        pair_copies.append(copy)
 
     barrier = pltpu.get_barrier_semaphore()
     signals = 0
@@ -216,6 +204,22 @@
     pl.semaphore_signal(barrier, inc=1, device_id={"pair": other}, device_id_type=MESH)
     signals += 1
 
+    loads = [
+        pltpu.make_async_copy(source, place, load_sem.at[k])
+        for k, (source, place) in enumerate(zip(sources, held))
+    ]
+    for copy in loads:
+        copy.start()
+    (frames, chain, mask, single, w_kv, w_kvp, c_fr, c_kp, c_kv) = held[:KEY_PATH]
+    (w_q, w_qp, w_pb, head_w, chain_b, gain, w_bb, w_out, c_q, c_qp, c_pa, c_perm, c_masks) = held[
+        KEY_PATH:
+    ]
+
+    for copy in loads[:KEY_PATH]:
+        copy.wait()
+    for o in order:
+        pltpu.make_async_copy(pair.at[:, block(o)], pv.at[:, slot_of[o]], pair_sem).start()
+
     stack[...] = jnp.zeros_like(stack)
     stack[0:12, :] = frames[...]
     stack[12:13, :] = chain[...].astype(F32)
@@ -229,8 +233,8 @@
     mine = pl.ds(pl.multiple_of(p * half, half), half)
     theirs = pl.ds(pl.multiple_of(other * half, half), half)
     ks = single[mine, :]
-    key_value = jnp.dot(ks, w_kv[...], preferred_element_type=F32)
-    key_local = jnp.dot(ks, w_kvp[...], preferred_element_type=F32)
+    key_value = lax.dot_general(ks, w_kv[...], NT, preferred_element_type=F32)
+    key_local = lax.dot_general(ks, w_kvp[...], NT, preferred_element_type=F32)
     turn = select(ft[mine, :], c_fr[...])
     local = select(key_local, c_kp[...])
     width = 2 * LANES
@@ -240,44 +244,38 @@
     buf[0, 0] = line[:, :LANES]
     buf[0, 1] = line[:, LANES:]
 
-    sends = []
-
     def relay(o):
         for child, delta in children.get(o, []):
-            copy = pltpu.make_async_remote_copy(
+            pltpu.make_async_remote_copy(
                 src_ref=buf.at[slot_of[o]],
                 dst_ref=buf.at[slot_of[child]],
-                send_sem=send_sem.at[slot_of[child]],
-                recv_sem=recv_sem.at[slot_of[child]],
+                send_sem=send_sem,
+                recv_sem=recv_sem.at[group_of[child]],
                 device_id={"blk": lax.rem(z + delta + n, n)},
                 device_id_type=MESH,
-            )
-            copy.start()
-            sends.append(copy)
-
-    arrived = set()
-
-    def arrive(o):
-        if o == 0 or o in arrived:
-            return
-        arrived.add(o)
+            ).start()
+
+    def arrive(first, last, group):
         pltpu.make_async_remote_copy(
-            src_ref=buf.at[slot_of[o]],
-            dst_ref=buf.at[slot_of[o]],
-            send_sem=send_sem.at[slot_of[o]],
-            recv_sem=recv_sem.at[slot_of[o]],
+            src_ref=buf.at[first:last],
+            dst_ref=buf.at[first:last],
+            send_sem=send_sem,
+            recv_sem=recv_sem.at[group],
             device_id={"blk": lax.rem(z + 1, n)},
             device_id_type=MESH,
         ).wait_recv()
-        relay(o)
 
     pl.semaphore_wait(barrier, signals)
     relay(0)
 
+    for copy in loads[KEY_PATH:]:
+        copy.wait()
     full = ft[...]
-    query = jnp.dot(single[...], w_q[...], preferred_element_type=F32)
+    query = lax.dot_general(single[...], w_q[...], NT, preferred_element_type=F32)
     query = select(query, c_q[...]) * (LW / math.sqrt(ch))
-    q_local = select(jnp.dot(single[...], w_qp[...], preferred_element_type=F32), c_qp[...])
+    q_local = select(
+        lax.dot_general(single[...], w_qp[...], NT, preferred_element_type=F32), c_qp[...]
+    )
     q_turn = select(full, c_fr[...])
     q_line = q_turn[:, 3 * width : 3 * width + LANES]
     for b in range(3):
@@ -294,23 +292,22 @@
     for k in range(marks):
         qpb[:, k] = jnp.broadcast_to(spread[:, :, k : k + 1], (rows, SUB, LANES))
 
-    head_row = lax.broadcasted_iota(jnp.int32, (SUB, LANES), 0)
-    raw = jnp.zeros((SUB, LANES), F32)
-    cross = jnp.zeros((SUB, LANES), F32)
-    for h in range(heads):
-        raw = jnp.where(head_row == h, head_w[h], raw)
-        cross = jnp.where(head_row == h, chain_b[h] * LW, cross)
+    diagonal = lax.broadcasted_iota(jnp.int32, (SUB, heads), 0) == lax.broadcasted_iota(
+        jnp.int32, (SUB, heads), 1
+    )
+
+    def down(row):
+        column = jnp.sum(jnp.where(diagonal, row, 0.0), axis=1, keepdims=True)
+        return jnp.broadcast_to(column, (SUB, LANES))
+
+    raw = down(head_w[...])
+    cross = down(chain_b[...]) * LW
     soft = jnp.maximum(raw, 0.0) + jnp.log1p(jnp.exp(-jnp.abs(raw)))
     near = soft * (LW * math.sqrt(2.0 / (9.0 * pq)) / 2.0)
 
-    eye_h = (
-        lax.broadcasted_iota(jnp.int32, (SUB, heads), 0)
-        == lax.broadcasted_iota(jnp.int32, (SUB, heads), 1)
-    ).astype(BF16)
-    w_bias = lax.dot_general(eye_h, w_pb[...], NT, preferred_element_type=F32).astype(BF16)
-
-    for copy in pair_copies:
-        copy.wait()
+    w_bias = jnp.dot(diagonal.astype(BF16), w_pb[...], preferred_element_type=F32).astype(BF16)
+
+    pltpu.make_async_copy(pair, pv, pair_sem).wait()
 
     keys = n * half
 
@@ -320,8 +317,7 @@
         )
         return 0
 
-    events = [o for o in order if children.get(o) and o != 0]
-    lax.fori_loop(0, rows, bias_of, 0, unroll=4)
+    lax.fori_loop(0, rows, bias_of, 0, unroll=8)
 
     short = w_out.shape[1] - LANES
     w_short = w_out[:, 0:short, :].reshape(heads * short, w_out.shape[2])
@@ -344,20 +340,24 @@
             picked = jnp.where(comp8 == k, wide[source : source + 1, :], picked)
         rsel[b] = picked
     eye_b = (
-        lax.broadcasted_iota(jnp.int32, (SUB, w_bb.shape[1]), 0)
-        == lax.broadcasted_iota(jnp.int32, (SUB, w_bb.shape[1]), 1)
+        lax.broadcasted_iota(jnp.int32, (SUB, w_bb.shape[0]), 0)
+        == lax.broadcasted_iota(jnp.int32, (SUB, w_bb.shape[0]), 1)
     ).astype(BF16)
-    w_motion = lax.dot_general(eye_b, w_bb[...], NT, preferred_element_type=F32).astype(BF16)
+    w_motion = jnp.dot(eye_b, w_bb[...], preferred_element_type=F32).astype(BF16)
+
+    for i, o in enumerate(anchors):
+        if o != 0:
+            arrive(i, i + 1, group_of[o])
+            relay(o)
 
     span = chunk * half
     acc[...] = jnp.zeros_like(acc)
     alpha[...] = jnp.full(alpha.shape, -1e30, F32)
     for c in range(n // chunk):
         slots = slice(c * chunk, (c + 1) * chunk)
-        for o in order[slots]:
-            arrive(o)
-        if c + 1 < n // chunk:
-            pass
+        first, last = max(len(anchors), c * chunk), (c + 1) * chunk
+        if first < last:
+            arrive(first, last, len(anchors) + c)
         kc = buf[slots, 0].reshape(span, LANES)
         vc = buf[slots, 1].reshape(span, LANES)
         kt[...] = kc.T.reshape(LANES // SUB, SUB, span)
@@ -395,7 +395,7 @@
             )
             return 0
 
-        lax.fori_loop(0, rows, one_row, 0, unroll=4)
+        lax.fori_loop(0, rows, one_row, 0, unroll=16)
         acc[:, 1] += jnp.dot(
             wts[...].reshape(rows * SUB, span), vc, precision=HIGH, preferred_element_type=F32
         ).reshape(rows, SUB, LANES)
@@ -445,37 +445,35 @@
         )
 
     xbuf[x] = update
-    x_copies = []
     for d in range(1, nx):
-        copy = pltpu.make_async_remote_copy(
+        pltpu.make_async_remote_copy(
             src_ref=xbuf.at[x],
             dst_ref=xbuf.at[x],
-            send_sem=x_send.at[d - 1],
-            recv_sem=x_recv.at[d - 1],
+            send_sem=x_sem.at[0],
+            recv_sem=x_sem.at[1],
             device_id={"head": lax.rem(x + d, nx)},
             device_id_type=MESH,
-        )
-        copy.start()
-        x_copies.append(copy)
-    for d in range(1, nx):
-        source = lax.rem(x - d + nx, nx)
-        pltpu.make_async_remote_copy(
-            src_ref=xbuf.at[source],
-            dst_ref=xbuf.at[source],
-            send_sem=x_send.at[d - 1],
-            recv_sem=x_recv.at[d - 1],
-            device_id={"head": source},
-            device_id_type=MESH,
-        ).wait_recv()
+        ).start()
+    x_all = pltpu.make_async_remote_copy(
+        src_ref=xbuf.at[0 : nx - 1],
+        dst_ref=xbuf.at[0 : nx - 1],
+        send_sem=x_sem.at[0],
+        recv_sem=x_sem.at[1],
+        device_id={"head": lax.rem(x + 1, nx)},
+        device_id_type=MESH,
+    )
+    if nx > 1:
+        x_all.wait_recv()
     update = xbuf[0]
     for k in range(1, nx):
         update = update + xbuf[k]
     mixed = single[mine, :].astype(F32) + update
     count = mixed.shape[1]
+    gains = jnp.concatenate([gain[k : k + 1, :] for k in range(count // LANES)], axis=1)
     centre = jnp.sum(mixed, axis=1, keepdims=True) * (1.0 / count)
     apart = mixed - centre
     variance = jnp.sum(apart * apart, axis=1, keepdims=True) * (1.0 / count)
-    result = (apart * lax.rsqrt(variance + 1e-05) * gain[...]).astype(BF16)
+    result = (apart * lax.rsqrt(variance + 1e-05) * gains).astype(BF16)
     out_single[mine, :] = result
     sbuf[0] = result.astype(F32)
     give_s = pltpu.make_async_remote_copy(
@@ -515,36 +513,32 @@
     me = z * 2 + p
     fbuf[me] = packed[0:lines, :]
 
-    f_copies = []
     steps = sorted(
         ((d, c) for d in range(n) for c in (0, 1) if (d, c) != (0, 0)),
         key=lambda s: (-min(s[0], n - s[0]), s[1]),
     )
     for d, c in steps:
         device = {"blk": lax.rem(z + d, n), "pair": p if c == 0 else other}
-        copy = pltpu.make_async_remote_copy(
+        pltpu.make_async_remote_copy(
             src_ref=fbuf.at[me],
             dst_ref=fbuf.at[me],
-            send_sem=f_send.at[2 * d + c],
-            recv_sem=f_recv.at[2 * d + c],
+            send_sem=f_sem.at[0],
+            recv_sem=f_sem.at[1],
             device_id=device,
             device_id_type=MESH,
-        )
-        copy.start()
-        f_copies.append(copy)
+        ).start()
     give_s.start()
     give_s.wait_recv()
     out_single[theirs, :] = sbuf[1].astype(BF16)
-    for d, c in reversed(steps):
-        source = lax.rem(z - d + n, n) * 2 + (p if c == 0 else other)
-        pltpu.make_async_remote_copy(
-            src_ref=fbuf.at[source],
-            dst_ref=fbuf.at[source],
-            send_sem=f_send.at[2 * d + c],
-            recv_sem=f_recv.at[2 * d + c],
-            device_id={"pair": other},
-            device_id_type=MESH,
-        ).wait_recv()
+    f_all = pltpu.make_async_remote_copy(
+        src_ref=fbuf.at[0 : 2 * n - 1],
+        dst_ref=fbuf.at[0 : 2 * n - 1],
+        send_sem=f_sem.at[0],
+        recv_sem=f_sem.at[1],
+        device_id={"pair": other},
+        device_id_type=MESH,
+    )
+    f_all.wait_recv()
 
     gap = (lax.broadcasted_iota(jnp.int32, (SUB, LANES), 0) - part8) & (SUB - 1)
     for t in range(2 * n // groups):
@@ -556,8 +550,17 @@
             height = 8 if line_number == 0 else 4
             out_frames[8 * line_number : 8 * line_number + height, t * LANES : (t + 1) * LANES] = out[:height]
 
-    for copy in sends + x_copies + f_copies:
-        copy.wait_send()
+    pltpu.make_async_remote_copy(
+        src_ref=buf.at[0 : n - 1],
+        dst_ref=buf.at[0 : n - 1],
+        send_sem=send_sem,
+        recv_sem=recv_sem.at[0],
+        device_id={"blk": lax.rem(z + 1, n)},
+        device_id_type=MESH,
+    ).wait_send()
+    if nx > 1:
+        x_all.wait_send()
+    f_all.wait_send()
     give.wait_send()
     give_s.wait_send()
 
@@ -585,24 +588,48 @@
     ch = w_q.shape[1] // heads
     pq = w_qp.shape[1] // (3 * heads)
     nv = w_kvp.shape[1] // (3 * heads) - pq
-    order, children = gather_plan(n, 6 if n >= 16 else 2, 0.9, 0.72, 0.4)
+    order, anchors, children = gather_plan(n, 6 if n >= 16 else 2, 0.9, 0.72, 0.4)
     deltas = sorted({d for kids in children.values() for _, d in kids})
     deltas = sorted(set(deltas) | {-d for d in deltas})
     deltas = [d for i, d in enumerate(deltas) if d % n not in {e % n for e in deltas[:i]}]
     chunk = min(8, n)
-    cfg = (n, nx, heads, ch, pq, nv, half, chunk, order, children, deltas)
+    cfg = (n, nx, heads, ch, pq, nv, half, chunk, order, anchors, children, deltas)
     hots, masks = constants(heads, ch, pq, nv)
     hots = [jnp.asarray(h, BF16) for h in hots]
     masks = jnp.asarray(masks, F32)
     vmem = pl.BlockSpec(memory_space=pltpu.VMEM)
-    smem = pl.BlockSpec(memory_space=pltpu.SMEM)
     hbm = pl.BlockSpec(memory_space=pl.ANY)
-    specs = [vmem, hbm, vmem, vmem, vmem, vmem, vmem, vmem, vmem, vmem, smem, smem]
-    specs += [vmem] * (3 + len(hots) + 1)
+    loads = [
+        frames,
+        chain.reshape(1, rows),
+        mask.reshape(1, rows),
+        single,
+        w_kv.T,
+        w_kvp.T,
+        hots[2],
+        hots[1],
+        hots[0],
+        w_q.T,
+        w_qp.T,
+        w_pb.T,
+        head_w.reshape(1, heads),
+        chain_b.reshape(1, heads),
+        gain.reshape(-1, LANES),
+        w_bb.T,
+        w_out,
+        hots[3],
+        hots[4],
+        hots[5],
+        hots[6],
+        masks,
+    ]
+    cfg += (len(loads),)
+    specs = [hbm] + [hbm] * len(loads)
     marks = 3 * pq + 2
     span = chunk * half
     width = w_out.shape[2]
-    scratch = [
+    scratch = [pltpu.VMEM(a.shape, a.dtype) for a in loads] + [
+        pltpu.SemaphoreType.DMA((len(loads),)),
         pltpu.VMEM((rows, n, half, LANES), BF16),
         pltpu.VMEM((n, 2, half, LANES), F32),
         pltpu.VMEM((16, rows), F32),
@@ -622,15 +649,13 @@
         pltpu.VMEM((2 * LANES, width), BF16),
         pltpu.VMEM((12, half, LANES), F32),
         pltpu.VMEM((4, SUB, LANES), F32),
-        pltpu.SemaphoreType.DMA((n,)),
-        pltpu.SemaphoreType.DMA((n,)),
-        pltpu.SemaphoreType.DMA((n,)),
+        pltpu.SemaphoreType.DMA,
+        pltpu.SemaphoreType.DMA,
+        pltpu.SemaphoreType.DMA((len(anchors) + -(-n // chunk),)),
         pltpu.SemaphoreType.DMA((2,)),
-        pltpu.SemaphoreType.DMA((max(nx - 1, 1),)),
-        pltpu.SemaphoreType.DMA((max(nx - 1, 1),)),
         pltpu.SemaphoreType.DMA((2,)),
-        pltpu.SemaphoreType.DMA((2 * n,)),
-        pltpu.SemaphoreType.DMA((2 * n,)),
+        pltpu.SemaphoreType.DMA((2,)),
+        pltpu.SemaphoreType.DMA((2,)),
     ]
     return pl.pallas_call(
         functools.partial(kernel, cfg),
@@ -643,25 +668,7 @@
         scratch_shapes=scratch,
         compiler_params=pltpu.CompilerParams(collective_id=0, has_side_effects=True),
         name="layer",
-    )(
-        single,
-        pair,
-        frames,
-        chain.reshape(1, rows),
-        mask.reshape(1, rows),
-        w_q,
-        w_kv,
-        w_qp,
-        w_kvp,
-        w_pb,
-        head_w,
-        chain_b,
-        w_out,
-        gain.reshape(1, -1),
-        w_bb,
-        *hots,
-        masks,
-    )
+    )(pair, *loads)
 
 
 def solution(mesh):

time: 120 us -> 92.3 us (0.77)
  Pallas kernels: 105 us -> 88.6 us
  local copies, waits for them, and re-layouts: 13.2 us -> 2.82 us
    pallas_call x1, Pallas kernels: 105 us -> 88.6 us  [body(): pl.pallas_call(functools.partial(kernel, cfg), out_shape=(jax.ShapeDtypeS...]
    unnamed x8 -> x2, local copies, waits for them, and re-layouts: 12 us -> 2.82 us
    reshape x1 -> x0, local copies, waits for them, and re-layouts: 1.25 us -> none  [body(): gain.reshape(1, -1)]
where the time goes in v2:
time: 92.3 us; the launch traced here: 92.1 us
  Pallas kernels  88.6 us (96%)
  local copies, waits for them, and re-layouts  2.82 us (3%)
    pallas_call x1, Pallas kernels, body(): pl.pallas_call(functools.partial(kernel, cfg), out_shape=(jax.ShapeDtypeS...  88.6 us
    unnamed x2, local copies, waits for them, and re-layouts  2.82 us

profile of v2, /device:TPU:33, one launch (start us, length us, event | category | flops | bytes accessed | tf_op | source)
XLA Modules:
  0.0 92.1 jit_solution(7968466958129958665)
XLA Ops:
  0.6 88.6 %layer.1 = (bf16[32,384]{1,0:T(8,128)(2,1)}, f32[12,1024]{1,0:T(8,128)}) custom-call(bf16[32,32,16,128]{3,2,1,0:T(8,128)(2,1)} %pair.1, f32[12,32]{1,0:T(8,128)} %refs_0_.1, s32[1,32]{1,0:T(1,128)} %bitcast.18, s32[1,32]{1,0:T(1,128)} %bitcast.19, bf16[32,384]{1,0:T(8,128)(2,1)} %refs_3_.1, bf16[96,384]{1,0:T(8,128)(2,1)} %bitcast.12, ...), custom_call_target="tpu_custom_call" | custom-call | tf_op jit(solution)/shard_map/layer/pallas_call | solution.py:660
  89.3 1.3 %copy.27 = bf16[32,384]{1,0:T(8,128)(2,1)} copy(bf16[32,384]{1,0:T(8,128)(2,1)} %get-tuple-element.4) | data formatting | bytes 49152
  90.6 1.5 %copy.28 = f32[12,1024]{1,0:T(8,128)} copy(f32[12,1024]{1,0:T(8,128)} %get-tuple-element.5) | data formatting | bytes 98304

commit v3 on v2

--- a/solution.py
+++ b/solution.py
@@ -16,6 +16,9 @@
 LW = math.sqrt(1.0 / 3.0)
 MASK_PENALTY = 100000.0
 KEY_PATH = 9
+PIECES = 7
+QUARTER = 4
+THIRD = 32
 LANES = 128
 SUB = 8
 NT = (((1,), (1,)), ((), ()))
@@ -26,7 +29,7 @@
 TOP_LANE = 121
 
 
-def gather_plan(n, stride, fixed, hop, weight):
+def gather_plan(n, stride, chunk, fixed, hop, weight):
     low, high = -((n - 1) // 2), n // 2
     when, parent = {0: 0.0}, {}
     anchors = [0]
@@ -47,8 +50,13 @@
         )
         parent[o] = (best, o - best)
         when[o] = when[best] + fixed + hop * abs(o - best)
-    order = sorted(when, key=lambda o: (o not in anchors, when[o], abs(o), o))
-    anchors = [o for o in order if o in anchors]
+    order = sorted(when, key=lambda o: (when[o], abs(o), o))
+    order = [
+        o
+        for c in range(0, n, chunk)
+        for o in sorted(order[c : c + chunk], key=lambda o: (o not in anchors, when[o]))
+    ]
+    anchors = sorted(anchors, key=lambda o: (when[o], -o))
     children = {}
     for o, (p, delta) in parent.items():
         children.setdefault(p, []).append((o, delta))
@@ -94,10 +102,11 @@
                 lane = vp_lane(h, p, a)
                 masks[2, h, lane] = 1
                 perm[lane, h * small + ch + p * 3 + a] = 1
+                line = 0 if lane >= 3 * THIRD else 1
                 for b in range(3):
-                    kp[(h * (pq + pv) + pq + p) * 3 + b, (2 * b + 1) * LANES + lane] = 1
-                    fr[3 * a + b, (2 * b + 1) * LANES + lane] = 1
-                fr[9 + a, 7 * LANES + lane] = 1
+                    kp[(h * (pq + pv) + pq + p) * 3 + b, (2 * b + line) * LANES + lane] = 1
+                    fr[3 * a + b, (2 * b + line) * LANES + lane] = 1
+                fr[9 + a, (6 + line) * LANES + lane] = 1
             perm[LANES + vp_lane(h, p, 0), h * small + ch + 3 * pv + p] = 1
     masks[1, :heads, CHAIN_LANE] = 1
     masks[1, :heads, MASK_LANE] = 1
@@ -105,7 +114,6 @@
     pa[MASK_LANE, 13] = 1
     fr[12, 6 * LANES + CHAIN_LANE] = 1
     fr[13, 6 * LANES + MASK_LANE] = 1
-    fr[14, 7 * LANES + ONE_LANE] = 1
     return (kv, kp, fr, q, qp, pa, perm), masks.reshape(3 * SUB, LANES)
 
 
@@ -149,6 +157,7 @@
     load_sem,
     pv,
     buf,
+    rbuf,
     stack,
     ft,
     bias,
@@ -182,20 +191,33 @@
     other = 1 - p
     slot_of = {o: i for i, o in enumerate(order)}
 
-    group_of = {o: i for i, o in enumerate(anchors)}
-    for i, o in enumerate(order[len(anchors) :], len(anchors)):
-        group_of[o] = len(anchors) + i // chunk
+    group_of = {o: len(anchors) + i // chunk for i, o in enumerate(order)}
+    group_of.update({o: i for i, o in enumerate(anchors)})
+    hub_slot = {o: i for i, o in enumerate(anchors)}
 
     def block(o):
         return lax.rem(z - o + 2 * n, n)
+
+    lane16 = lax.broadcasted_iota(jnp.int32, (half, LANES), 1)
+
+    loads = [
+        pltpu.make_async_copy(source, place, load_sem.at[k])
+        for k, (source, place) in enumerate(zip(sources, held))
+    ]
+    for copy in loads[:KEY_PATH]:
+        copy.start()
 
     barrier = pltpu.get_barrier_semaphore()
     signals = 0
     for d in deltas:
-        pl.semaphore_signal(
-            barrier, inc=1, device_id={"blk": lax.rem(z + d + n, n)}, device_id_type=MESH
-        )
-        signals += 1
+        for core in (p, other):
+            pl.semaphore_signal(
+                barrier,
+                inc=1,
+                device_id={"blk": lax.rem(z + d + n, n), "pair": core},
+                device_id_type=MESH,
+            )
+            signals += 1
     for d in range(1, nx):
         pl.semaphore_signal(
             barrier, inc=1, device_id={"head": lax.rem(x + d, nx)}, device_id_type=MESH
@@ -204,11 +226,7 @@
     pl.semaphore_signal(barrier, inc=1, device_id={"pair": other}, device_id_type=MESH)
     signals += 1
 
-    loads = [
-        pltpu.make_async_copy(source, place, load_sem.at[k])
-        for k, (source, place) in enumerate(zip(sources, held))
-    ]
-    for copy in loads:
+    for copy in loads[KEY_PATH:]:
         copy.start()
     (frames, chain, mask, single, w_kv, w_kvp, c_fr, c_kp, c_kv) = held[:KEY_PATH]
     (w_q, w_qp, w_pb, head_w, chain_b, gain, w_bb, w_out, c_q, c_qp, c_pa, c_perm, c_masks) = held[
@@ -224,7 +242,6 @@
     stack[0:12, :] = frames[...]
     stack[12:13, :] = chain[...].astype(F32)
     stack[13:14, :] = mask[...].astype(F32)
-    stack[14:15, :] = jnp.ones((1, rows), F32)
     eye = (
         lax.broadcasted_iota(jnp.int32, (rows, rows), 0)
         == lax.broadcasted_iota(jnp.int32, (rows, rows), 1)
@@ -241,32 +258,74 @@
     line = select(key_value, c_kv[...]) + turn[:, 3 * width :]
     for b in range(3):
         line += turn[:, b * width : (b + 1) * width] * local[:, b * width : (b + 1) * width]
-    buf[0, 0] = line[:, :LANES]
-    buf[0, 1] = line[:, LANES:]
+    near_line = line[:, :LANES]
+    for k in range(4):
+        buf[k] = near_line[QUARTER * k : QUARTER * (k + 1)]
+    far_line = line[:, LANES:]
+    last_rows = far_line[3 * QUARTER :]
+    lane4 = lax.broadcasted_iota(jnp.int32, (QUARTER, LANES), 1)
+    for k in range(3):
+        moved_rows = roll(last_rows, 3 * THIRD - k * THIRD, 1)
+        buf[4 + k] = jnp.where(
+            lane4 < 3 * THIRD, far_line[QUARTER * k : QUARTER * (k + 1)], moved_rows
+        )
+
+    def send(src, place, group, delta, core, sem):
+        pltpu.make_async_remote_copy(
+            src_ref=src,
+            dst_ref=place,
+            send_sem=send_sem.at[sem],
+            recv_sem=recv_sem.at[group],
+            device_id={"blk": lax.rem(z + delta + n, n), "pair": core},
+            device_id_type=MESH,
+        ).start()
+
+    def held_block(ref, first, last=None):
+        last = first + 1 if last is None else last
+        return ref.at[first * PIECES : last * PIECES]
 
     def relay(o):
         for child, delta in children.get(o, []):
-            pltpu.make_async_remote_copy(
-                src_ref=buf.at[slot_of[o]],
-                dst_ref=buf.at[slot_of[child]],
-                send_sem=send_sem,
-                recv_sem=recv_sem.at[group_of[child]],
-                device_id={"blk": lax.rem(z + delta + n, n)},
-                device_id_type=MESH,
-            ).start()
-
-    def arrive(first, last, group):
+            send(held_block(buf, slot_of[o]), held_block(buf, slot_of[child]), group_of[child], delta, p, 0)
+
+    hub_group = {o: len(anchors) + n // chunk + i for i, o in enumerate(anchors)}
+
+    def hub_relay(o):
+        src = held_block(rbuf, hub_slot[o])
+        for child, delta in children.get(o, []):
+            if child in anchors:
+                send(src, held_block(rbuf, hub_slot[child]), hub_group[child], delta, 1, 1)
+            else:
+                send(src, held_block(buf, slot_of[child]), group_of[child], delta, 0, 1)
+        send(src, held_block(buf, slot_of[o]), group_of[o], 0, 0, 1)
+
+    def first_sends():
+        for child, delta in children[0]:
+            if child in anchors:
+                send(held_block(buf, 0), held_block(rbuf, hub_slot[child]), hub_group[child], delta, 1, 0)
+            else:
+                send(held_block(buf, 0), held_block(buf, slot_of[child]), group_of[child], delta, 0, 0)
+
+    def take(ref, first, last, group):
         pltpu.make_async_remote_copy(
-            src_ref=buf.at[first:last],
-            dst_ref=buf.at[first:last],
-            send_sem=send_sem,
+            src_ref=held_block(ref, first, last),
+            dst_ref=held_block(ref, first, last),
+            send_sem=send_sem.at[0],
             recv_sem=recv_sem.at[group],
             device_id={"blk": lax.rem(z + 1, n)},
             device_id_type=MESH,
         ).wait_recv()
 
     pl.semaphore_wait(barrier, signals)
-    relay(0)
+
+    @pl.when(p == 1)
+    def _():
+        relay(0)
+
+    @pl.when(p == 0)
+    def _():
+        first_sends()
+
 
     for copy in loads[KEY_PATH:]:
         copy.wait()
@@ -285,7 +344,10 @@
     head_keys = c_masks[0:SUB, :]
     head_points = c_masks[SUB : 2 * SUB, :]
     head_values = c_masks[2 * SUB : 3 * SUB, :]
-    qblk[...] = (query[:, None, :] * head_keys[None]).reshape(rows * SUB, LANES)
+    wide_query = (query[:, None, :] * head_keys[None]).reshape(rows * SUB, LANES)
+    coarse = wide_query.astype(BF16)
+    qblk[0] = coarse
+    qblk[1] = (wide_query - coarse.astype(F32)).astype(BF16)
     spread = select((q_line[:, None, :] * head_points[None]).reshape(rows * SUB, LANES), c_pa[...])
     spread = spread.reshape(rows, SUB, LANES)
     marks = 3 * pq + 2
@@ -345,25 +407,60 @@
     ).astype(BF16)
     w_motion = jnp.dot(eye_b, w_bb[...], preferred_element_type=F32).astype(BF16)
 
-    for i, o in enumerate(anchors):
-        if o != 0:
-            arrive(i, i + 1, group_of[o])
-            relay(o)
+    def unpacked(slot):
+        piece = [buf[slot * PIECES + k] for k in range(PIECES)]
+        near_line = jnp.concatenate(piece[:4], axis=0)
+        tail = jnp.zeros((QUARTER, LANES), F32)
+        lane4 = lax.broadcasted_iota(jnp.int32, (QUARTER, LANES), 1)
+        for k in range(3):
+            tail = jnp.where(
+                (lane4 >= k * THIRD) & (lane4 < (k + 1) * THIRD), roll(piece[4 + k], k * THIRD - 3 * THIRD, 1), tail
+            )
+        far_line = jnp.concatenate(piece[4:] + [tail], axis=0)
+        far_line = jnp.where(lane16 < 3 * THIRD, far_line, near_line)
+        return near_line, jnp.where(lane16 == ONE_LANE, 1.0, far_line)
 
     span = chunk * half
     acc[...] = jnp.zeros_like(acc)
     alpha[...] = jnp.full(alpha.shape, -1e30, F32)
+    def pass_on(these):
+        @pl.when(p == 1)
+        def _():
+            for reach in sorted({abs(o) for o in these}):
+                level = [o for o in these if abs(o) == reach]
+                for o in level:
+                    take(buf, slot_of[o], slot_of[o] + 1, group_of[o])
+                    relay(o)
+                for o in level:
+                    take(rbuf, hub_slot[o], hub_slot[o] + 1, hub_group[o])
+                    hub_relay(o)
+
+        @pl.when(p == 0)
+        def _():
+            for o in these:
+                take(buf, slot_of[o], slot_of[o] + 1, group_of[o])
+
+    late = [o for o in anchors if o not in order[:chunk] and abs(o) == max(abs(a) for a in anchors)]
+    pass_on([o for o in anchors if o != 0 and o not in late])
     for c in range(n // chunk):
+        if c == min(2, n // chunk - 1):
+            pass_on(late)
         slots = slice(c * chunk, (c + 1) * chunk)
-        first, last = max(len(anchors), c * chunk), (c + 1) * chunk
+        first = c * chunk + sum(o in anchors for o in order[slots])
+        last = (c + 1) * chunk
         if first < last:
-            arrive(first, last, len(anchors) + c)
-        kc = buf[slots, 0].reshape(span, LANES)
-        vc = buf[slots, 1].reshape(span, LANES)
+            take(buf, first, last, len(anchors) + c)
+        lines = [unpacked(slot) for slot in range(c * chunk, (c + 1) * chunk)]
+        kc = jnp.concatenate([a for a, _ in lines], axis=0)
+        vc = jnp.concatenate([b for _, b in lines], axis=0)
         kt[...] = kc.T.reshape(LANES // SUB, SUB, span)
-        dots[...] = lax.dot_general(
-            qblk[...], kc, NT, precision=HIGH, preferred_element_type=F32
-        ).reshape(rows, SUB, span)
+        k_coarse = kc.astype(BF16)
+        k_fine = (kc - k_coarse.astype(F32)).astype(BF16)
+        products = [
+            lax.dot_general(a, b, NT, preferred_element_type=F32)
+            for a, b in ((qblk[0], k_coarse), (qblk[0], k_fine), (qblk[1], k_coarse))
+        ]
+        dots[...] = (products[0] + products[1] + products[2]).reshape(rows, SUB, span)
         chain_j = kt[0, 7:8, :]
         mask_j = kt[1, 7:8, :]
 
@@ -395,7 +492,7 @@
             )
             return 0
 
-        lax.fori_loop(0, rows, one_row, 0, unroll=16)
+        lax.fori_loop(0, rows, one_row, 0, unroll=rows)
         acc[:, 1] += jnp.dot(
             wts[...].reshape(rows * SUB, span), vc, precision=HIGH, preferred_element_type=F32
         ).reshape(rows, SUB, LANES)
@@ -428,7 +525,6 @@
     moved = [roll(sums, -a * third, 1) - rb[9 + a] for a in range(3)]
     pointed = [sum(rb[3 * a + b] * moved[a] for a in range(3)) for b in range(3)]
     norms = jnp.sqrt(pointed[0] * pointed[0] + pointed[1] * pointed[1] + pointed[2] * pointed[2] + 1.0)
-    lane16 = lax.broadcasted_iota(jnp.int32, (half, LANES), 1)
     joined = sums
     for b in range(3):
         joined = jnp.where(
@@ -550,14 +646,25 @@
             height = 8 if line_number == 0 else 4
             out_frames[8 * line_number : 8 * line_number + height, t * LANES : (t + 1) * LANES] = out[:height]
 
-    pltpu.make_async_remote_copy(
-        src_ref=buf.at[0 : n - 1],
-        dst_ref=buf.at[0 : n - 1],
-        send_sem=send_sem,
-        recv_sem=recv_sem.at[0],
-        device_id={"blk": lax.rem(z + 1, n)},
-        device_id_type=MESH,
-    ).wait_send()
+    def sent(count, sem):
+        pltpu.make_async_remote_copy(
+            src_ref=held_block(buf, 0, count),
+            dst_ref=held_block(buf, 0, count),
+            send_sem=send_sem.at[sem],
+            recv_sem=recv_sem.at[0],
+            device_id={"blk": lax.rem(z + 1, n)},
+            device_id_type=MESH,
+        ).wait_send()
+
+    @pl.when(p == 1)
+    def _():
+        sent(n - 1, 0)
+        sent(n - 1 - len(children[0]) + len(anchors) - 1, 1)
+
+    @pl.when(p == 0)
+    def _():
+        sent(len(children[0]), 0)
+
     if nx > 1:
         x_all.wait_send()
     f_all.wait_send()
@@ -588,11 +695,11 @@
     ch = w_q.shape[1] // heads
     pq = w_qp.shape[1] // (3 * heads)
     nv = w_kvp.shape[1] // (3 * heads) - pq
-    order, anchors, children = gather_plan(n, 6 if n >= 16 else 2, 0.9, 0.72, 0.4)
+    chunk = min(8, n)
+    order, anchors, children = gather_plan(n, 4 if n >= 16 else 2, chunk, 0.9, 0.72, 1.0)
     deltas = sorted({d for kids in children.values() for _, d in kids})
     deltas = sorted(set(deltas) | {-d for d in deltas})
     deltas = [d for i, d in enumerate(deltas) if d % n not in {e % n for e in deltas[:i]}]
-    chunk = min(8, n)
     cfg = (n, nx, heads, ch, pq, nv, half, chunk, order, anchors, children, deltas)
     hots, masks = constants(heads, ch, pq, nv)
     hots = [jnp.asarray(h, BF16) for h in hots]
@@ -631,12 +738,13 @@
     scratch = [pltpu.VMEM(a.shape, a.dtype) for a in loads] + [
         pltpu.SemaphoreType.DMA((len(loads),)),
         pltpu.VMEM((rows, n, half, LANES), BF16),
-        pltpu.VMEM((n, 2, half, LANES), F32),
+        pltpu.VMEM((n * PIECES, QUARTER, LANES), F32),
+        pltpu.VMEM((len(anchors) * PIECES, QUARTER, LANES), F32),
         pltpu.VMEM((16, rows), F32),
         pltpu.VMEM((rows, 16), F32),
         pltpu.VMEM((rows, SUB, n * half), F32),
         pltpu.VMEM((rows, marks, SUB, LANES), F32),
-        pltpu.VMEM((rows * SUB, LANES), F32),
+        pltpu.VMEM((2, rows * SUB, LANES), BF16),
         pltpu.VMEM((LANES // SUB, SUB, span), F32),
         pltpu.VMEM((rows, SUB, span), F32),
         pltpu.VMEM((rows, SUB, span), F32),
@@ -650,8 +758,8 @@
         pltpu.VMEM((12, half, LANES), F32),
         pltpu.VMEM((4, SUB, LANES), F32),
         pltpu.SemaphoreType.DMA,
-        pltpu.SemaphoreType.DMA,
-        pltpu.SemaphoreType.DMA((len(anchors) + -(-n // chunk),)),
+        pltpu.SemaphoreType.DMA((2,)),
+        pltpu.SemaphoreType.DMA((2 * len(anchors) + n // chunk,)),
         pltpu.SemaphoreType.DMA((2,)),
         pltpu.SemaphoreType.DMA((2,)),
         pltpu.SemaphoreType.DMA((2,)),

time: 92.3 us -> 88.2 us (0.956)
  Pallas kernels: 88.6 us -> 84.5 us
    pallas_call x1, Pallas kernels: 88.6 us -> 84.5 us  [body(): pl.pallas_call(functools.partial(kernel, cfg), out_shape=(jax.ShapeDtypeS...]
where the time goes in v3:
time: 88.2 us; the launch traced here: 88 us
  Pallas kernels  84.5 us (96%)
  local copies, waits for them, and re-layouts  2.82 us (3%)
    pallas_call x1, Pallas kernels, body(): pl.pallas_call(functools.partial(kernel, cfg), out_shape=(jax.ShapeDtypeS...  84.5 us
    unnamed x2, local copies, waits for them, and re-layouts  2.82 us

profile of v3, /device:TPU:33, one launch (start us, length us, event | category | flops | bytes accessed | tf_op | source)
XLA Modules:
  0.0 88.0 jit_solution(15014057079660684017)
XLA Ops:
  0.6 84.5 %layer.1 = (bf16[32,384]{1,0:T(8,128)(2,1)}, f32[12,1024]{1,0:T(8,128)}) custom-call(bf16[32,32,16,128]{3,2,1,0:T(8,128)(2,1)} %pair.1, f32[12,32]{1,0:T(8,128)} %refs_0_.1, s32[1,32]{1,0:T(1,128)} %bitcast.18, s32[1,32]{1,0:T(1,128)} %bitcast.19, bf16[32,384]{1,0:T(8,128)(2,1)} %refs_3_.1, bf16[96,384]{1,0:T(8,128)(2,1)} %bitcast.12, ...), custom_call_target="tpu_custom_call" | custom-call | tf_op jit(solution)/shard_map/layer/pallas_call | solution.py:768
  85.2 1.3 %copy.27 = bf16[32,384]{1,0:T(8,128)(2,1)} copy(bf16[32,384]{1,0:T(8,128)(2,1)} %get-tuple-element.4) | data formatting | bytes 49152
  86.5 1.5 %copy.28 = f32[12,1024]{1,0:T(8,128)} copy(f32[12,1024]{1,0:T(8,128)} %get-tuple-element.5) | data formatting | bytes 98304

commit v4 on v3

--- a/solution.py
+++ b/solution.py
@@ -670,6 +670,11 @@
     f_all.wait_send()
     give.wait_send()
     give_s.wait_send()
+
+
+def hand_over(single_in, frames_in, single_out, frames_out):
+    single_out[...] = single_in[...]
+    frames_out[...] = frames_in[...]
 
 
 def body(n, nx, *args):
@@ -765,7 +770,7 @@
         pltpu.SemaphoreType.DMA((2,)),
         pltpu.SemaphoreType.DMA((2,)),
     ]
-    return pl.pallas_call(
+    results = pl.pallas_call(
         functools.partial(kernel, cfg),
         out_shape=(
             jax.ShapeDtypeStruct(single.shape, BF16),
@@ -777,6 +782,16 @@
         compiler_params=pltpu.CompilerParams(collective_id=0, has_side_effects=True),
         name="layer",
     )(pair, *loads)
+    return pl.pallas_call(
+        hand_over,
+        out_shape=(
+            jax.ShapeDtypeStruct(single.shape, BF16),
+            jax.ShapeDtypeStruct((12, n * rows), F32),
+        ),
+        in_specs=[vmem, vmem],
+        out_specs=(vmem, vmem),
+        name="results",
+    )(*results)
 
 
 def solution(mesh):

time: 88.2 us -> 86.9 us (0.985)
  local copies, waits for them, and re-layouts: 2.82 us -> 0 us
  Pallas kernels: 84.5 us -> 86 us
    unnamed x2 -> x0, local copies, waits for them, and re-layouts: 2.82 us -> none
    pallas_call x0 -> x1, Pallas kernels: none -> 1.5 us  [body(): pl.pallas_call(hand_over, out_shape=(jax.ShapeDtypeStruct(single.shape, B...]
where the time goes in v4:
time: 86.9 us; the launch traced here: 86.7 us
  Pallas kernels  86 us (99%)
    pallas_call x1, Pallas kernels, body(): pl.pallas_call(functools.partial(kernel, cfg), out_shape=(jax.ShapeDtypeS...  84.5 us

profile of v4, /device:TPU:33, one launch (start us, length us, event | category | flops | bytes accessed | tf_op | source)
XLA Modules:
  0.0 86.7 jit_solution(13869036539780895261)
XLA Ops:
  0.6 84.5 %layer.1 = (bf16[32,384]{1,0:T(8,128)(2,1)}, f32[12,1024]{1,0:T(8,128)}) custom-call(bf16[32,32,16,128]{3,2,1,0:T(8,128)(2,1)} %pair.1, f32[12,32]{1,0:T(8,128)} %refs_0_.1, s32[1,32]{1,0:T(1,128)} %bitcast.18, s32[1,32]{1,0:T(1,128)} %bitcast.19, bf16[32,384]{1,0:T(8,128)(2,1)} %refs_3_.1, bf16[96,384]{1,0:T(8,128)(2,1)} %bitcast.12, ...), custom_call_target="tpu_custom_call" | custom-call | tf_op jit(solution)/shard_map/layer/pallas_call | solution.py:773
  85.2 1.5 %results.1 = (bf16[32,384]{1,0:T(8,128)(2,1)}, f32[12,1024]{1,0:T(8,128)}) custom-call(bf16[32,384]{1,0:T(8,128)(2,1)} %get-tuple-element.4.single_in, f32[12,1024]{1,0:T(8,128)} %get-tuple-element.5.frames_in), custom_call_target="tpu_custom_call" | custom-call | tf_op jit(solution)/shard_map/results/pallas_call | solution.py:785

commit v5 on v4

--- a/solution.py
+++ b/solution.py
@@ -200,16 +200,9 @@
 
     lane16 = lax.broadcasted_iota(jnp.int32, (half, LANES), 1)
 
-    loads = [
-        pltpu.make_async_copy(source, place, load_sem.at[k])
-        for k, (source, place) in enumerate(zip(sources, held))
-    ]
-    for copy in loads[:KEY_PATH]:
-        copy.start()
-
     barrier = pltpu.get_barrier_semaphore()
-    signals = 0
-    for d in deltas:
+    near_first = sorted(deltas, key=abs)
+    for d in near_first[-2:]:
         for core in (p, other):
             pl.semaphore_signal(
                 barrier,
@@ -217,15 +210,31 @@
                 device_id={"blk": lax.rem(z + d + n, n), "pair": core},
                 device_id_type=MESH,
             )
-            signals += 1
+
+    loads = [
+        pltpu.make_async_copy(source, place, load_sem.at[k])
+        for k, (source, place) in enumerate(zip(sources, held))
+    ]
+    for copy in loads[:KEY_PATH]:
+        copy.start()
+
+    def greet(d, core):
+        pl.semaphore_signal(
+            barrier,
+            inc=1,
+            device_id={"blk": lax.rem(z + d + n, n), "pair": core},
+            device_id_type=MESH,
+        )
+
+    for d in near_first[:-2]:
+        for core in (p, other):
+            greet(d, core)
     for d in range(1, nx):
         pl.semaphore_signal(
             barrier, inc=1, device_id={"head": lax.rem(x + d, nx)}, device_id_type=MESH
         )
-        signals += 1
     pl.semaphore_signal(barrier, inc=1, device_id={"pair": other}, device_id_type=MESH)
-    signals += 1
-
+    signals = 2 * len(deltas) + nx
     for copy in loads[KEY_PATH:]:
         copy.start()
     (frames, chain, mask, single, w_kv, w_kvp, c_fr, c_kp, c_kv) = held[:KEY_PATH]
@@ -541,7 +550,7 @@
         )
 
     xbuf[x] = update
-    for d in range(1, nx):
+    for d in sorted(range(1, nx), key=lambda d: -min(d, nx - d)):
         pltpu.make_async_remote_copy(
             src_ref=xbuf.at[x],
             dst_ref=xbuf.at[x],

time: 86.9 us -> 86.7 us (level)
  no operation moved by 1% of the time
where the time goes in v5:
time: 86.7 us; the launch traced here: 86.5 us
  Pallas kernels  85.9 us (99%)
    pallas_call x1, Pallas kernels, body(): pl.pallas_call(functools.partial(kernel, cfg), out_shape=(jax.ShapeDtypeS...  84.4 us

profile of v5, /device:TPU:33, one launch (start us, length us, event | category | flops | bytes accessed | tf_op | source)
XLA Modules:
  0.0 86.5 jit_solution(5436894056771971724)
XLA Ops:
  0.6 84.4 %layer.1 = (bf16[32,384]{1,0:T(8,128)(2,1)}, f32[12,1024]{1,0:T(8,128)}) custom-call(bf16[32,32,16,128]{3,2,1,0:T(8,128)(2,1)} %pair.1, f32[12,32]{1,0:T(8,128)} %refs_0_.1, s32[1,32]{1,0:T(1,128)} %bitcast.18, s32[1,32]{1,0:T(1,128)} %bitcast.19, bf16[32,384]{1,0:T(8,128)(2,1)} %refs_3_.1, bf16[96,384]{1,0:T(8,128)(2,1)} %bitcast.12, ...), custom_call_target="tpu_custom_call" | custom-call | tf_op jit(solution)/shard_map/layer/pallas_call | solution.py:782
  85.0 1.5 %results.1 = (bf16[32,384]{1,0:T(8,128)(2,1)}, f32[12,1024]{1,0:T(8,128)}) custom-call(bf16[32,384]{1,0:T(8,128)(2,1)} %get-tuple-element.4.single_in, f32[12,1024]{1,0:T(8,128)} %get-tuple-element.5.frames_in), custom_call_target="tpu_custom_call" | custom-call | tf_op jit(solution)/shard_map/results/pallas_call | solution.py:794

commit v6 on v4

--- a/solution.py
+++ b/solution.py
@@ -493,9 +493,21 @@
             return 0
 
         lax.fori_loop(0, rows, one_row, 0, unroll=rows)
-        acc[:, 1] += jnp.dot(
-            wts[...].reshape(rows * SUB, span), vc, precision=HIGH, preferred_element_type=F32
-        ).reshape(rows, SUB, LANES)
+        w_all = wts[...].reshape(rows * SUB, span)
+        w_coarse = w_all.astype(BF16)
+        w_fine = (w_all - w_coarse.astype(F32)).astype(BF16)
+        v_first, v_second, v_third = pieces3(vc)
+        value_sums = [
+            jnp.dot(a, b, preferred_element_type=F32)
+            for a, b in (
+                (w_coarse, v_third),
+                (w_fine, v_second),
+                (w_coarse, v_second),
+                (w_fine, v_first),
+                (w_coarse, v_first),
+            )
+        ]
+        acc[:, 1] += sum(value_sums[1:], value_sums[0]).reshape(rows, SUB, LANES)
 
     lane3 = lax.broadcasted_iota(jnp.int32, (rows, SUB, LANES), 2)
     acc[:, 1] = jnp.where(lane3 == TOP_LANE, alpha[...], acc[:, 1])

time: 86.9 us -> 86.8 us (level)
  no operation moved by 1% of the time
where the time goes in v6:
time: 86.8 us; the launch traced here: 86.6 us
  Pallas kernels  86 us (99%)
    pallas_call x1, Pallas kernels, body(): pl.pallas_call(functools.partial(kernel, cfg), out_shape=(jax.ShapeDtypeS...  84.5 us

profile of v6, /device:TPU:33, one launch (start us, length us, event | category | flops | bytes accessed | tf_op | source)
XLA Modules:
  0.0 86.6 jit_solution(5125783147857580638)
XLA Ops:
  0.6 84.5 %layer.1 = (bf16[32,384]{1,0:T(8,128)(2,1)}, f32[12,1024]{1,0:T(8,128)}) custom-call(bf16[32,32,16,128]{3,2,1,0:T(8,128)(2,1)} %pair.1, f32[12,32]{1,0:T(8,128)} %refs_0_.1, s32[1,32]{1,0:T(1,128)} %bitcast.18, s32[1,32]{1,0:T(1,128)} %bitcast.19, bf16[32,384]{1,0:T(8,128)(2,1)} %refs_3_.1, bf16[96,384]{1,0:T(8,128)(2,1)} %bitcast.12, ...), custom_call_target="tpu_custom_call" | custom-call | tf_op jit(solution)/shard_map/layer/pallas_call | solution.py:785
  85.1 1.5 %results.1 = (bf16[32,384]{1,0:T(8,128)(2,1)}, f32[12,1024]{1,0:T(8,128)}) custom-call(bf16[32,384]{1,0:T(8,128)(2,1)} %get-tuple-element.4.single_in, f32[12,1024]{1,0:T(8,128)} %get-tuple-element.5.frames_in), custom_call_target="tpu_custom_call" | custom-call | tf_op jit(solution)/shard_map/results/pallas_call | solution.py:797
